TPU v7x, 256 devices: a 8x8x2 block of a 8x8x16 slice. The times are simulated.
256 devices in a mesh: groups: 2 (over z), dev: 128 (over x, y, core).
Axes of the slice: x: 8, y: 8, z: 2, core: 2. Of those that a mesh axis runs over, the one named last changes fastest.
The devices are a block of a 8x8x16 slice.
Arguments:
- tokens: bfloat16 [1024, 6144], P(('groups', 'dev')), parts along dimension 0, may hold values from -6 to 6
- queries: bfloat16 [1024, 6144], P(('groups', 'dev')), parts along dimension 0, may hold values from -250 to 250
- token_kv: bfloat16 [1024, 2048], P(('groups', 'dev')), parts along dimension 0, may hold values from -6 to 6
- kv_cache: bfloat16 [1024, 64, 2048], P(('groups', 'dev')), parts along dimension 0, may hold values from -6.5 to 6.5, as said below
- context_lengths: int32 [1024], P(('groups', 'dev')), parts along dimension 0, may hold values from 2 to 64
- fresh_kv: bfloat16 [16384, 2048], P(('groups', 'dev')), parts along dimension 0, may hold values from -6 to 6
- block_counts: int32 [256], P('groups'), parts along dimension 0, may hold values from 0 to 8, as said below
- expert_ids: int32 [1024, 2], P(('groups', 'dev')), parts along dimension 0, may hold values from 0 to 3, all different within a row; in each aligned block of 4 rows (0 to 3, 4 to 7, ...) at most 3 rows name the same one
- route_weights: float32 [1024, 2], P(('groups', 'dev')), parts along dimension 0, may hold values from 0.25 to 1
- norm_gain: float32 [6144], replicated, may hold values from 0.1 to 1.9
- w_gate: bfloat16 [6144, 32768], P(None, 'dev'), may hold values from -0.078125 to 0.078125
- w_up: bfloat16 [6144, 32768], P(None, 'dev'), may hold values from -0.078125 to 0.078125
- w_down: bfloat16 [32768, 6144], P('dev'), may hold values from -0.0625 to 0.0625
Outputs:
- layer_out: bfloat16 [1024, 6144], P(('groups', 'dev')), parts along dimension 0
There are 2 independent parts, one for each index of `groups`. A program takes and returns all parts, laid end to end along the dimension named above; an argument that names none is the same for every part. Nothing has to cross between parts.
Inputs may be any that keep to these rules, and one draw needn't show every extreme that they name: `kv_cache`: each request's cached keys and values; the table of arrays gives their range. `block_counts`: the counts sum to 512; for every device d > 0 the exclusive prefix sum before it lies between d * 4 + 1 and (d + 1) * 4; the first device takes 2 * 4 blocks. `expert_ids`: among the rows of one device no expert is named more than 3 times, and in some devices one expert is named exactly 3 times.
All inputs are finite; a program needn't handle non-finite values.
Results may differ from a plain program's by a relative error of at most 0.008.
Values may be sent and summed in bfloat16 or wider, within the bound.
A program may use at most 128 MiB of HBM per device.

v0:
```python
import math

import jax
import jax.numpy as jnp
from jax import lax
from jax.sharding import Mesh
from jax.sharding import PartitionSpec as P

QH = 48
KVH = 8
HD = 128
EXPERTS = 4
BLOCK = 16
MOST = 3
DEV = ("dev_0", "dev_1", "dev_2")
GROUPS_DEV = ("groups", "dev_0", "dev_1", "dev_2")


EPS = 1e-05
NEG = -1e30


def passed_along(value, axis, steps):
    count = lax.axis_size(axis)
    leading, last = (max(0, -steps), min(count, count - steps))
    return lax.ppermute(value, axis, [(source, source + steps) for source in range(leading, last)])


def split_up(shard, dim, devices):
    dims = shard.shape
    parts = shard.reshape(*dims[:dim], devices, dims[dim] // devices, *dims[dim + 1 :])
    return jnp.moveaxis(parts, dim, 0)


def joined_along(parts, dim):
    parts = jnp.moveaxis(parts, 0, dim)
    dims = parts.shape
    return parts.reshape(*dims[:dim], dims[dim] * dims[dim + 1], *dims[dim + 2 :])


def turned_blocks(parts, axes, order):
    inside = parts.shape[1:]
    out = parts.reshape(*(lax.axis_size(a) for a in axes), *inside)
    for k in order:
        out = lax.all_to_all(out, axes[k], k, k, tiled=True)
    return out.reshape(-1, *inside)


def exchange_by_chip(shard, groups, order, split_dim, concat_dim):
    devices = lax.axis_size(groups[0]) * lax.axis_size(groups[1])
    parts = split_up(shard, split_dim, devices)
    return joined_along(turned_blocks(parts, groups, order), concat_dim)


def gather_in_order(shard, axes, order):
    parts = shard[None]
    for k in order:
        parts = lax.all_gather(parts, axes[k], axis=0, tiled=True)
    carried = [lax.axis_size(axes[k]) for k in reversed(order)]
    parts = parts.reshape(*carried, *shard.shape)
    turned = sorted(range(len(order)), key=lambda place: order[len(order) - 1 - place])
    return parts.transpose(*turned, *range(len(order), parts.ndim)).reshape(-1, *shard.shape)


def gather_axes(shard, axes, order, dim):
    return joined_along(gather_in_order(shard, axes, order), dim)


def attend(query, cache, lens, own, window, first, last):
    reqs = query.shape[0]
    length = cache.shape[1]
    group = QH // KVH
    half = KVH * HD
    scale = 1.0 / math.sqrt(HD)
    q_all = query.reshape(reqs, KVH, group, HD)
    keys_c = cache[:, :, :half].reshape(reqs, length, KVH, HD)
    vals_c = cache[:, :, half:].reshape(reqs, length, KVH, HD)
    keys_w = window[:, :half].reshape(-1, KVH, HD)
    vals_w = window[:, half:].reshape(-1, KVH, HD)
    keys_o = own[:, :half].reshape(reqs, KVH, HD)
    vals_o = own[:, half:].astype(jnp.float32).reshape(reqs, KVH, HD)
    s_cache = (
        jnp.einsum("rkgh,rpkh->rkgp", q_all, keys_c, preferred_element_type=jnp.float32) * scale
    )
    places = jnp.arange(length, dtype=jnp.int32)
    s_cache = jnp.where(places[None, None, None, :] < lens[:, None, None, None], s_cache, NEG)
    s_win = jnp.einsum("rkgh,pkh->rkgp", q_all, keys_w, preferred_element_type=jnp.float32) * scale
    rows = jnp.arange(window.shape[0], dtype=jnp.int32)
    live = (rows >= first) & (rows < last)
    leader = jnp.arange(reqs, dtype=jnp.int32) == 0
    usable = leader[:, None] & live[None, :]
    s_win = jnp.where(usable[:, None, None, :], s_win, NEG)
    s_own = jnp.einsum("rkgh,rkh->rkg", q_all, keys_o, preferred_element_type=jnp.float32) * scale
    top = jnp.maximum(jnp.maximum(jnp.max(s_cache, -1), jnp.max(s_win, -1)), s_own)
    e_cache = jnp.exp(s_cache - top[..., None])
    e_win = jnp.exp(s_win - top[..., None])
    e_own = jnp.exp(s_own - top)
    total = jnp.sum(e_cache, -1) + jnp.sum(e_win, -1) + e_own
    p_cache = (e_cache / total[..., None]).astype(jnp.bfloat16)
    p_win = (e_win / total[..., None]).astype(jnp.bfloat16)
    p_own = (e_own / total).astype(jnp.bfloat16).astype(jnp.float32)
    mixed = jnp.einsum("rkgp,rpkh->rkgh", p_cache, vals_c, preferred_element_type=jnp.float32)
    mixed = mixed + jnp.einsum("rkgp,pkh->rkgh", p_win, vals_w, preferred_element_type=jnp.float32)
    mixed = mixed + p_own[..., None] * vals_o[:, :, None, :]
    return mixed.reshape(reqs, QH * HD)


def per_device(
    tokens,
    queries,
    token_kv,
    kv_cache,
    context_lengths,
    fresh_kv,
    block_counts,
    expert_ids,
    route_weights,
    norm_gain,
    w_gate,
    w_up,
    w_down,
):
    devices = lax.axis_size(DEV)
    me = lax.axis_index(DEV)
    reqs = tokens.shape[0]
    width = tokens.shape[1]
    span = fresh_kv.shape[0]
    following = passed_along(fresh_kv, DEV, -1)
    window = jnp.concatenate([fresh_kv, following], 0)
    offsets = jnp.cumsum(block_counts) - block_counts
    mine = lax.dynamic_index_in_dim(offsets, me, 0, keepdims=False)
    taken = lax.dynamic_index_in_dim(block_counts, me, 0, keepdims=False)
    first = (mine - me * (span // BLOCK)) * BLOCK
    last = first + taken * BLOCK
    attn = attend(queries, kv_cache, context_lengths, token_kv, window, first, last)
    hidden_state = tokens.astype(jnp.float32) + attn
    spread = jnp.mean(hidden_state * hidden_state, -1, keepdims=True)
    normed = (hidden_state * lax.rsqrt(spread + EPS) * norm_gain).astype(jnp.bfloat16)
    shards = devices // EXPERTS
    labels = jnp.arange(EXPERTS, dtype=jnp.int32)
    flat_ids = expert_ids.reshape(-1)
    picks = (flat_ids[:, None] == labels[None, :]).astype(jnp.int32)
    slots = jnp.sum((jnp.cumsum(picks, 0) - picks) * picks, 1)
    cells = flat_ids * MOST + slots
    cell_ids = jnp.arange(EXPERTS * MOST, dtype=jnp.int32)
    every_row = lax.all_gather(normed, DEV, axis=0, tiled=True)
    every_id = gather_axes(expert_ids, DEV, (0, 1, 2), 0)
    source_ids = every_id.reshape(devices, reqs * 2)
    picks_all = (source_ids[:, :, None] == labels[None, None, :]).astype(jnp.int32)
    slots_all = jnp.sum((jnp.cumsum(picks_all, 1) - picks_all) * picks_all, 2)
    target = me // shards
    hit = source_ids == target
    slot_ids = jnp.arange(MOST, dtype=jnp.int32)
    taking = hit[:, None, :] & (slots_all[:, None, :] == slot_ids[None, :, None])
    taking_rows = jnp.sum(taking.reshape(devices, MOST, reqs, 2).astype(jnp.float32), 3).astype(
        jnp.bfloat16
    )
    arrived = jnp.einsum(
        "smt,std->smd",
        taking_rows,
        every_row.reshape(devices, reqs, width),
        preferred_element_type=jnp.float32,
    ).astype(jnp.bfloat16)
    sources, items, cols = arrived.shape
    rows = arrived.reshape(sources * items, cols)
    gate_v = jnp.dot(rows, w_gate, preferred_element_type=jnp.float32)
    up_v = jnp.dot(rows, w_up, preferred_element_type=jnp.float32)
    act = (jax.nn.silu(gate_v) * up_v).astype(jnp.bfloat16)
    part = jnp.dot(act, w_down, preferred_element_type=jnp.float32).astype(jnp.bfloat16)
    merged = jnp.sum(
        exchange_by_chip(
            part.reshape(sources, items, cols), (("dev_0", "dev_1"), "dev_2"), (1, 0), 0, 0
        )
        .reshape(EXPERTS, shards, MOST, width)
        .astype(jnp.float32),
        1,
    ).reshape(EXPERTS * MOST, width)
    pairs = cells.reshape(reqs, 2)
    mixing = jnp.sum(
        route_weights[:, :, None]
        * (pairs[:, :, None] == cell_ids[None, None, :]).astype(jnp.float32),
        1,
    )
    moe = jnp.dot(mixing, merged, preferred_element_type=jnp.float32)
    return (hidden_state + moe).astype(jnp.bfloat16)


def solution(mesh):
    split = Mesh(
        mesh.devices.reshape(mesh.shape["groups"], 8, 8, 2), ("groups", "dev_0", "dev_1", "dev_2")
    )
    return jax.shard_map(
        per_device,
        mesh=split,
        in_specs=(
            P(GROUPS_DEV, None),
            P(GROUPS_DEV, None),
            P(GROUPS_DEV, None),
            P(GROUPS_DEV, None, None),
            P(GROUPS_DEV),
            P(GROUPS_DEV, None),
            P("groups"),
            P(GROUPS_DEV, None),
            P(GROUPS_DEV, None),
            P(),
            P(None, DEV),
            P(None, DEV),
            P(DEV, None),
        ),
        out_specs=P(GROUPS_DEV, None),
        check_vma=False,
    )
```

profile of v0, /device:TPU:516, one launch (start us, length us, event | category | flops | bytes accessed | tf_op | source)
XLA Modules:
  0.0 378.9 jit_solution(13576945794137781858)
XLA Ops:
  6.6 2.1 copy.158
  8.7 13.3 %collective-permute-start = (bf16[64,2048]{0,1:T(8,128)(2,1)}, bf16[64,2048]{0,1:T(8,128)(2,1)}, u32[]{:S(2)}, u32[]{:S(2)}) collective-permute-start(bf16[64,2048]{0,1:T(8,128)(2,1)} %copy.158), channel_id=1, source_target_pairs={{1,0},{2,1},{3,2},{4,3},{5,4},{6,5},{7,6},{8,7},{9,8},{10,9},{11,1... | collective-permute-start | bytes 786440 | tf_op jit(solution)/shard_map/ppermute | solution.py:26
  23.7 1.3 dynamic_slice.8
  27.8 2.3 slice_bitcast_fusion.1
  31.8 1.5 fusion.34
  33.3 1.5 pad_maximum_fusion
  35.6 1.3 fusion.7
  39.8 18.1 %all-gather.1 = s32[8,4,2]{1,2,0:T(2,128)S(1)} all-gather(s32[1,4,2]{1,2,0:T(2,128)S(1)} %bitcast.81), channel_id=2, replica_groups=mesh['groups'=2,'dev_0'=8,'dev_1'=8,'dev_2'=2] {'dev_0'}, dimensions={0}, use_global_device_ids=true | all-gather | bytes 288 | tf_op jit(solution)/shard_map/all_gather | solution.py:58
  57.9 24.6 %all_gather.13 = s32[64,4,2]{1,2,0:T(2,128)S(1)} all-gather(s32[8,4,2]{1,2,0:T(2,128)S(1)} %all-gather.1), channel_id=1, replica_groups=mesh['groups'=2,'dev_0'=8,'dev_1'=8,'dev_2'=2] {'dev_1'}, dimensions={0}, use_global_device_ids=true | all-gather | bytes 2304 | tf_op jit(solution)/shard_map/all_gather | solution.py:58
  82.5 2.1 all_gather.14
  84.9 1.7 copy.189
  88.7 40.3 %all-gather.5.cloned.1.call-done = bf16[128,4,6144]{2,1,0:T(4,128)(2,1)} async-done(((bf16[1,4,6144]{2,1,0:T(4,128)(2,1)}), bf16[128,4,6144]{2,1,0:T(4,128)(2,1)}) %all-gather.5.cloned.1.call-update) | async-done | bytes 6291472 | tf_op jit(solution)/shard_map/all_gather | solution.py:146
  129.0 8.2 %convolution_convert_fusion = bf16[128,3,6144]{2,1,0:T(4,128)(2,1)} fusion(bf16[128,3,4]{2,1,0:T(4,128)(2,1)S(1)} %copy.176, bf16[128,4,6144]{2,1,0:T(4,128)(2,1)} %all-gather.5.cloned.1.call-done), kind=kOutput, calls=%fused_computation.1 | convolution fusion | flops 21233664 | bytes 11013120 | tf_op jit(solution)/shard_map/smt,std->smd/dot_general | solution.py:158
  137.2 12.3 %reshape.164 = bf16[384,6144]{1,0:T(8,128)(2,1)} reshape(bf16[128,3,6144]{2,1,0:T(4,128)(2,1)} %convolution_convert_fusion) | data formatting | bytes 9437184 | tf_op jit(solution)/shard_map/reshape | solution.py:165
  149.5 5.5 %fusion.37 = f32[384,256]{1,0:T(8,128)} fusion(bf16[384,6144]{1,0:T(8,128)(2,1)} %reshape.164, bf16[6144,256]{1,0:T(8,128)(2,1)} %param.23), kind=kOutput, calls=%fused_computation.78 | convolution fusion | flops 1207959552 | bytes 8257536 | tf_op jit(solution)/shard_map/dot_general | solution.py:166
  155.0 10.6 %convolution_convert_fusion.1 = bf16[384,6144]{1,0:T(8,128)(2,1)} fusion(bf16[256,6144]{1,0:T(8,128)(2,1)S(1)} %copy-done, bf16[384,6144]{1,0:T(8,128)(2,1)} %reshape.164, bf16[6144,256]{1,0:T(8,128)(2,1)} %param.24, f32[384,256]{1,0:T(8,128)} %fusion.37), kind=kOutput, calls=%fused_computation.2 | convolution fusion | flops 2418868224 | bytes 16121856 | tf_op jit(solution)/shard_map/dot_general | solution.py:169
  165.5 11.7 %reshape_reshape_reshape.2 = bf16[64,2,1,3,6144]{4,3,1,0,2:T(4,128)(2,1)} reshape(bf16[384,6144]{1,0:T(8,128)(2,1)} %convolution_convert_fusion.1) | data formatting | bytes 9437184 | tf_op jit(solution)/shard_map/reshape;reshape;reshape | solution.py:43
  177.3 6.2 %copy.177 = bf16[64,2,1,3,6144]{4,0,3,2,1:T(8,128)(2,1)S(1)} copy(bf16[64,2,1,3,6144]{4,3,1,0,2:T(4,128)(2,1)} %reshape_reshape_reshape.2) | data formatting | bytes 9437184 | tf_op jit(solution)/shard_map/reshape;reshape;reshape | solution.py:43
  183.5 8.7 %all_to_all.10 = bf16[64,2,1,3,6144]{4,0,3,2,1:T(8,128)(2,1)} all-to-all(bf16[64,2,1,3,6144]{4,0,3,2,1:T(8,128)(2,1)S(1)} %copy.177), channel_id=1, replica_groups=mesh['groups'=2,'dev_0'=8,'dev_1'=8,'dev_2'=2] {'dev_2'}, dimensions={1} | all-to-all | bytes 9437184 | tf_op jit(solution)/shard_map/all_to_all | solution.py:45
  192.1 9.3 %copy.178 = bf16[64,2,1,3,6144]{4,1,3,2,0:T(2,128)(2,1)} copy(bf16[64,2,1,3,6144]{4,0,3,2,1:T(8,128)(2,1)} %all_to_all.10) | data formatting | bytes 9437184 | tf_op jit(solution)/shard_map/all_to_all | solution.py:45
  201.4 10.1 %all-to-all-start.1 = ((bf16[64,2,1,3,6144]{4,1,3,2,0:T(2,128)(2,1)}), bf16[64,2,1,3,6144]{4,1,3,2,0:T(2,128)(2,1)}, u32[]{:S(2)}, u32[]{:S(2)}) async-start(bf16[64,2,1,3,6144]{4,1,3,2,0:T(2,128)(2,1)} %copy.178), calls=%async_computation.1 | async-start | bytes 9437184 | tf_op jit(solution)/shard_map/all_to_all | solution.py:45
  212.2 140.5 %all-to-all-done.1 = bf16[64,2,1,3,6144]{4,1,3,2,0:T(2,128)(2,1)} async-done(((bf16[64,2,1,3,6144]{4,1,3,2,0:T(2,128)(2,1)}), bf16[64,2,1,3,6144]{4,1,3,2,0:T(2,128)(2,1)}, u32[]{:S(2)}, u32[]{:S(2)}) %all-to-all-start.1) | async-done | bytes 4718624 | tf_op jit(solution)/shard_map/all_to_all | solution.py:45
  352.8 16.1 %convert_reduce_fusion = f32[64,3,6144]{2,1,0:T(4,128)S(1)} fusion(bf16[64,2,1,3,6144]{4,1,3,2,0:T(2,128)(2,1)} %all-to-all-done.1), kind=kLoop, calls=%fused_computation | loop fusion | flops 3538944 | bytes 9437184 | tf_op jit(solution)/shard_map/reduce_sum | solution.py:170
  370.4 1.7 fusion
  (63 shorter events, 13.0 us)
Async XLA Ops:
  6.5 148.4 %copy-start = (bf16[256,6144]{1,0:T(8,128)(2,1)S(1)}, bf16[256,6144]{1,0:T(8,128)(2,1)}, u32[]{:S(2)}) copy-start(bf16[256,6144]{1,0:T(8,128)(2,1)} %param.25) | copy-start | bytes 9437188
  6.6 32.3 %copy-start.2 = (bf16[4,6144]{1,0:T(4,128)(2,1)S(1)}, bf16[4,6144]{1,0:T(4,128)(2,1)}, u32[]{:S(2)}) copy-start(bf16[4,6144]{1,0:T(4,128)(2,1)} %param.13) | copy-start | bytes 147460
  6.6 32.4 %copy-start.3 = (f32[6144]{0:T(1024)S(1)}, f32[6144]{0:T(1024)}, u32[]{:S(2)}) copy-start(f32[6144]{0:T(1024)} %param.22) | copy-start | bytes 73732
  6.6 122.4 %all-gather.5.cloned.1.call-start = ((), (), s32[]{:S(2)}) async-start(), calls=%async_computation.2 | async-start | bytes 6340608 | tf_op jit(solution)/shard_map/all_gather | solution.py:146
  8.7 31.1 %copy-start.4 = (s32[4,2]{0,1:T(2,128)S(1)}, s32[4,2]{0,1:T(2,128)}, u32[]{:S(2)}) copy-start(s32[4,2]{0,1:T(2,128)} %param.20) | copy-start | bytes 100
  8.7 24.6 %collective-permute-start = (bf16[64,2048]{0,1:T(8,128)(2,1)}, bf16[64,2048]{0,1:T(8,128)(2,1)}, u32[]{:S(2)}, u32[]{:S(2)}) collective-permute-start(bf16[64,2048]{0,1:T(8,128)(2,1)} %copy.158), channel_id=1, source_target_pairs={{1,0},{2,1},{3,2},{4,3},{5,4},{6,5},{7,6},{8,7},{9,8},{10,9},{11,1... | collective-permute-start | bytes 786440 | tf_op jit(solution)/shard_map/ppermute | solution.py:26
  201.4 10.7 %copy-start.5 = (f32[4,2]{0,1:T(2,128)S(1)}, f32[4,2]{0,1:T(2,128)}, u32[]{:S(2)}) copy-start(f32[4,2]{0,1:T(2,128)} %param.21) | copy-start | bytes 100
  201.4 151.3 %all-to-all-start.1 = ((bf16[64,2,1,3,6144]{4,1,3,2,0:T(2,128)(2,1)}), bf16[64,2,1,3,6144]{4,1,3,2,0:T(2,128)(2,1)}, u32[]{:S(2)}, u32[]{:S(2)}) async-start(bf16[64,2,1,3,6144]{4,1,3,2,0:T(2,128)(2,1)} %copy.178), calls=%async_computation.1 | async-start | bytes 9437184 | tf_op jit(solution)/shard_map/all_to_all | solution.py:45
  352.8 19.3 %copy-start.1 = (bf16[256,6144]{1,0:T(8,128)(2,1)S(1)}, bf16[256,6144]{1,0:T(8,128)(2,1)}, u32[]{:S(2)}) copy-start(bf16[256,6144]{1,0:T(8,128)(2,1)} %param.25) | copy-start | bytes 9437188
Sparse Core Ops, SparseCore 0:
  39.9 89.0 all-gather.4
where the time goes:
time: 381 us; the launch traced here: 379 us
  waiting for transfers between devices  181 us (48%)
  local copies, waits for them, and re-layouts  53.6 us (14%)
  blocking collectives  53.5 us (14%)
  matrix products  30.1 us (8%)
  starting transfers between devices  23.4 us (6%)
  other arithmetic  22.5 us (6%)
  between operations  15 us (4%)
    all_to_all x1, waiting for transfers between devices, turned_blocks(): out = lax.all_to_all(out, axes[k], k, k, tiled=True)  141 us
    all_gather x3, blocking collectives, gather_in_order(): parts = lax.all_gather(parts, axes[k], axis=0, tiled=True)  44.8 us
    all_gather x1, waiting for transfers between devices, per_device(): every_row = lax.all_gather(normed, DEV, axis=0, tiled=True)  40.3 us
    another operation x2, local copies, waits for them, and re-layouts, turned_blocks(): out = parts.reshape(*(lax.axis_size(a) for a in axes), *inside)  17.9 us
    reduce_sum x2, other arithmetic, per_device(): jnp.sum(exchange_by_chip(part.reshape(sources, items, cols), (('dev_0', '...  16.8 us
    ppermute x1, starting transfers between devices, passed_along(): lax.ppermute(value, axis, [(source, source + steps) for source in range(l...  13.3 us
    reshape x1, local copies, waits for them, and re-layouts, per_device(): rows = arrived.reshape(sources * items, cols)  12.3 us
    dot_general x1, matrix products, per_device(): jnp.dot(act, w_down, preferred_element_type=jnp.float32)  10.6 us
  transfers between devices with their start and end apart: 3, of which 2 were waited for; matrix products, arithmetic and copies ran while one was open for 4% of the time, Pallas kernels for 0%

commit v1 on v0

v1 whole, which is shorter than its diff:
```python
import math

import jax
import jax.numpy as jnp
from jax import lax
from jax.sharding import Mesh
from jax.sharding import PartitionSpec as P
from jax.experimental import pallas as pl
from jax.experimental.pallas import tpu as pltpu

QH = 48
KVH = 8
HD = 128
EXPERTS = 4
BLOCK = 16
DEV = ("dev_0", "dev_1", "dev_2")
GROUPS_DEV = ("groups", "dev_0", "dev_1", "dev_2")


EPS = 1e-05
NEG = -1e30


def passed_along(value, axis, steps):
    count = lax.axis_size(axis)
    leading, last = (max(0, -steps), min(count, count - steps))
    return lax.ppermute(value, axis, [(source, source + steps) for source in range(leading, last)])


MESH_ID = pl.DeviceIdType.MESH
RING = ("dev_1", "dev_0")
LINE = ("dev_0", "dev_1")
SUBS = 2


def exchange_kernel(
    rows_ref, coef_ref, perm_ref, back_ref, gate_hbm, up_hbm, down_hbm, out_ref,
    gathered, coefs, wide, act, part, crossed, hops, fin, w_gate, w_up, w_down,
    sem_w, c_send, c_recv, g1_send, g1_recv, g2_send, g2_recv, gx_send, gx_recv,
    x_send, x_recv, r_send, r_recv, f_send, f_recv,
):
    n = lax.axis_size("dev_0")
    half_n = n // 2
    core = lax.axis_index("dev_2")
    other = 1 - core
    sgn = 1 - 2 * core
    xy = {"dev_0": lax.axis_index("dev_0"), "dev_1": lax.axis_index("dev_1")}
    pos = [xy[a] for a in RING]
    line = [xy[a] for a in LINE]
    width = rows_ref.shape[2]
    per = n // SUBS

    def wrap(v):
        return lax.rem(v + 2 * n, n)

    loads = [
        pltpu.make_async_copy(src, dst, sem_w.at[i])
        for i, (src, dst) in enumerate(((gate_hbm, w_gate), (up_hbm, w_up), (down_hbm, w_down)))
    ]
    for load in loads:
        load.start()

    barrier = pltpu.get_barrier_semaphore()
    pl.semaphore_signal(barrier, inc=1, device_id={"dev_2": other}, device_id_type=MESH_ID)
    for axis in LINE:
        for j in range(1, n):
            pl.semaphore_signal(
                barrier, inc=1, device_id={axis: wrap(xy[axis] + j)}, device_id_type=MESH_ID
            )
    pl.semaphore_wait(barrier, 2 * (n - 1) + 1)

    pending = []

    def send(src, dst, s_sem, r_sem, where):
        copy = pltpu.make_async_remote_copy(
            src_ref=src, dst_ref=dst, send_sem=s_sem, recv_sem=r_sem,
            device_id=where, device_id_type=MESH_ID,
        )
        copy.start()
        pending.append(copy)
        return copy

    gathered[0, core, pos[0], line[0]] = rows_ref[0]
    gathered[1, core, pos[1], line[1]] = rows_ref[1]
    coefs[core, xy["dev_1"], xy["dev_0"]] = coef_ref[0]
    firsts = []
    for j in range(1, n):
        firsts.append(
            send(
                coef_ref.at[0], coefs.at[core, xy["dev_1"], xy["dev_0"]], c_send.at[j], c_recv.at[j],
                {"dev_0": wrap(xy["dev_0"] + j)},
            )
        )
        for h in range(2):
            firsts.append(
                send(
                    rows_ref.at[h], gathered.at[h, core, pos[h], line[h]],
                    g1_send.at[h, j], g1_recv.at[h, j], {LINE[h]: wrap(line[h] + j)},
                )
            )
    for copy in firsts:
        copy.wait_recv()
    seconds = []
    for j in range(1, n):
        seconds.append(
            send(
                coefs.at[core, xy["dev_1"]], coefs.at[core, xy["dev_1"]],
                c_send.at[n + j], c_recv.at[n + j], {"dev_1": wrap(xy["dev_1"] + j)},
            )
        )

    crossing = []

    def cross(h, where, sub, slot):
        ref = gathered.at[h, core, where, pl.ds(sub * per, per)]
        crossing.append(
            send(ref, ref, gx_send.at[h, slot, sub], gx_recv.at[h, slot, sub], {"dev_2": other})
        )

    last = {}
    for s in range(1, half_n + 1):
        for sub in range(SUBS):
            for h in range(2):
                for way, hops_of in ((0, half_n), (1, half_n - 1)):
                    if s > hops_of:
                        continue
                    turn = sgn if way == 0 else -sgn
                    where = wrap(pos[h] - turn * (s - 1))
                    if s > 1:
                        last[h, way, sub].wait_recv()
                    ref = gathered.at[h, core, where, pl.ds(sub * per, per)]
                    last[h, way, sub] = send(
                        ref, ref, g2_send.at[h, way, s - 1, sub], g2_recv.at[h, way, s - 1, sub],
                        {RING[h]: wrap(pos[h] + turn)},
                    )
                    if s > 1:
                        cross(h, where, sub, way * half_n + s - 1)
                    elif way == 0:
                        cross(h, where, sub, 0)
    for sub in range(SUBS):
        for h in range(2):
            for way, hops_of in ((0, half_n), (1, half_n - 1)):
                turn = sgn if way == 0 else -sgn
                last[h, way, sub].wait_recv()
                cross(h, wrap(pos[h] - turn * hops_of), sub, way * half_n + hops_of)
    for copy in seconds:
        copy.wait_recv()
    both = send(coefs.at[core], coefs.at[core], c_send.at[0], c_recv.at[0], {"dev_2": other})
    both.wait_recv()
    for copy in crossing:
        copy.wait_recv()
    for load in loads:
        load.wait()

    expert = (xy["dev_0"] * (2 * n) + xy["dev_1"] * 2 + core) // (2 * n * n // EXPERTS)
    toks = 4
    batch = 2 * n * toks
    batches = n // 2
    tile = 256

    def spread(i, carry):
        cc = jnp.where(i < batches, other, core)
        yp = lax.rem(i, batches) * 2
        for t in range(width // tile):
            cols = pl.ds(t * tile, tile)
            for h in range(2):
                if h == 0:
                    z = gathered[0, cc, pl.ds(yp, 2), :, :, cols].reshape(4 * batch, tile)
                else:
                    z = jnp.concatenate(
                        [
                            gathered[1, cc, :, yp + k, :, cols].reshape(2 * batch, tile)
                            for k in range(2)
                        ],
                        0,
                    )
                z = jnp.dot(perm_ref[...], z, preferred_element_type=jnp.float32).astype(jnp.bfloat16)
                for q in range(4):
                    wide[pl.ds(i * batch, batch), pl.ds((2 * q + h) * width + t * tile, tile)] = z[
                        q * batch : (q + 1) * batch
                    ]
        return carry

    lax.fori_loop(0, 2 * batches, spread, 0)

    def experts(i, carry):
        at = pl.ds(i * 4 * batch, 4 * batch)
        cc = jnp.where(i < 1, other, core)
        gate = jnp.dot(wide[at], w_gate[...], preferred_element_type=jnp.float32)
        up = jnp.dot(wide[at], w_up[...], preferred_element_type=jnp.float32)
        sub8 = lax.broadcasted_iota(jnp.int32, (8, 128), 0)
        lane8 = lax.broadcasted_iota(jnp.int32, (8, 128), 1)
        keep = lane8 == lax.rem(sub8, toks) * EXPERTS + expert
        pieces = []
        for y in range(n):
            for x in range(0, n, 2):
                both = jnp.where(sub8 < toks, coefs[cc, y, x], coefs[cc, y, x + 1])
                pieces.append(jnp.sum(jnp.where(keep, both, 0.0), 1, keepdims=True))
        coef = jnp.concatenate(pieces, 0)
        act[at] = (gate / (1.0 + jnp.exp(-gate)) * up * coef).astype(jnp.bfloat16)
        return carry

    lax.fori_loop(0, 2, experts, 0)

    crossed_copies = []
    for turn in range(2):
        cc = other if turn == 0 else core
        at = pl.ds(turn * 4 * batch, 4 * batch)

        def down(t, carry):
            cols = pl.ds(pl.multiple_of(t * tile, tile), tile)
            wide[at, cols] = jnp.dot(
                act[at], w_down[:, cols], preferred_element_type=jnp.float32
            ).astype(jnp.bfloat16)
            return carry

        lax.fori_loop(0, wide.shape[1] // tile, down, 0)

        def gathered_back(i, carry):
            rows = pl.ds((turn * batches + i) * batch, batch)
            yp = 2 * i
            for t in range(width // tile):
                cols = pl.ds(t * tile, tile)
                for h in range(2):
                    z = jnp.concatenate(
                        [
                            wide[rows, pl.ds((2 * q + h) * width + t * tile, tile)]
                            for q in range(4)
                        ],
                        0,
                    )
                    z = jnp.dot(back_ref[...], z, preferred_element_type=jnp.float32)
                    z = z.astype(jnp.bfloat16).reshape(2, n, 16, tile)
                    if h == 0:
                        part[0, cc, pl.ds(yp, 2), :, :, cols] = z
                    else:
                        for k in range(2):
                            part[1, cc, :, yp + k, :, cols] = z[k]
            return carry

        lax.fori_loop(0, batches, gathered_back, 0)
        if turn == 0:
            for h in range(2):
                for k in range(batches):
                    at_k = pl.ds(2 * k, 2)
                    crossed_copies.append(
                        send(
                            part.at[h, other, at_k], crossed.at[h, at_k],
                            x_send.at[h, k], x_recv.at[h, k], {"dev_2": other},
                        )
                    )
    for copy in crossed_copies:
        copy.wait_recv()

    held = {}
    for s in range(1, half_n + 1):
        for sub in range(SUBS):
            for h in range(2):
                for way, hops_of in ((0, half_n), (1, half_n - 1)):
                    if s > hops_of:
                        continue
                    turn = sgn if way == 0 else -sgn
                    dest = wrap(pos[h] + turn * (hops_of + 1 - s))
                    at = pl.ds(sub * per, per)
                    total = part[h, core, dest, at].astype(jnp.float32) + crossed[
                        h, dest, at
                    ].astype(jnp.float32)
                    if s > 1:
                        held[h, way, sub].wait_recv()
                        total = total + hops[h, way, s - 2, at].astype(jnp.float32)
                    part[h, core, dest, at] = total.astype(jnp.bfloat16)
                    held[h, way, sub] = send(
                        part.at[h, core, dest, at], hops.at[h, way, s - 1, at],
                        r_send.at[h, way, s - 1, sub], r_recv.at[h, way, s - 1, sub],
                        {RING[h]: wrap(pos[h] + turn)},
                    )
    finals = []
    for sub in range(SUBS):
        for h in range(2):
            at = pl.ds(sub * per, per)
            total = part[h, core, pos[h], at].astype(jnp.float32) + crossed[h, pos[h], at].astype(
                jnp.float32
            )
            for way, hops_of in ((0, half_n), (1, half_n - 1)):
                held[h, way, sub].wait_recv()
                total = total + hops[h, way, hops_of - 1, at].astype(jnp.float32)
            part[h, core, pos[h], at] = total.astype(jnp.bfloat16)
    for j in range(1, n):
        for h in range(2):
            finals.append(
                send(
                    part.at[h, core, pos[h], wrap(line[h] + j)], fin.at[h, j],
                    f_send.at[h, j], f_recv.at[h, j], {LINE[h]: wrap(line[h] + j)},
                )
            )
    for copy in finals:
        copy.wait_recv()
    for h in range(2):
        total = part[h, core, pos[h], line[h]].astype(jnp.float32)
        for j in range(1, n):
            total = total + fin[h, j].astype(jnp.float32)
        out_ref[h] = total
    for copy in pending:
        copy.wait_send()


def exchange(rows, coef, w_gate, w_up, w_down):
    n = lax.axis_size("dev_0")
    width = rows.shape[2]
    full = w_gate.shape[0]
    units = w_gate.shape[1]
    tokens = 2 * n * n * 4
    size = 4 * 2 * n * 4
    r = jnp.arange(size, dtype=jnp.int32)
    q, b, t = r // (size // 4), (r // 4) % (size // 16), r % 4
    source = b * 16 + q * 4 + t
    perm = (source[:, None] == r[None, :]).astype(jnp.bfloat16)
    back = perm.T
    vmem = pl.BlockSpec(memory_space=pltpu.VMEM)
    anyspace = pl.BlockSpec(memory_space=pl.ANY)
    bf = jnp.bfloat16
    dma = pltpu.SemaphoreType.DMA
    half_n = n // 2
    return pl.pallas_call(
        exchange_kernel,
        out_shape=jax.ShapeDtypeStruct(rows.shape, jnp.float32),
        in_specs=[vmem] * 4 + [anyspace] * 3,
        out_specs=vmem,
        scratch_shapes=[
            pltpu.VMEM((2, 2, n, n, 16, width), bf),
            pltpu.VMEM((2, n, n, 1, 128), jnp.float32),
            pltpu.VMEM((tokens, full), bf),
            pltpu.VMEM((tokens, units), bf),
            pltpu.VMEM((2, 2, n, n, 16, width), bf),
            pltpu.VMEM((2, n, n, 16, width), bf),
            pltpu.VMEM((2, 2, half_n, n, 16, width), bf),
            pltpu.VMEM((2, n, 16, width), bf),
            pltpu.VMEM(w_gate.shape, bf),
            pltpu.VMEM(w_up.shape, bf),
            pltpu.VMEM(w_down.shape, bf),
            dma((3,)),
            dma((2 * n,)), dma((2 * n,)),
            dma((2, n)), dma((2, n)),
            dma((2, 2, half_n, SUBS)), dma((2, 2, half_n, SUBS)),
            dma((2, 2 * half_n, SUBS)), dma((2, 2 * half_n, SUBS)),
            dma((2, n // 2)), dma((2, n // 2)),
            dma((2, 2, half_n, SUBS)), dma((2, 2, half_n, SUBS)),
            dma((2, n)), dma((2, n)),
        ],
        compiler_params=pltpu.CompilerParams(
            collective_id=0, has_side_effects=True, vmem_limit_bytes=58 * 1024 * 1024
        ),
    )(rows, coef, perm, back, w_gate, w_up, w_down)


def attend(query, cache, lens, own, window, first, last):
    reqs = query.shape[0]
    length = cache.shape[1]
    group = QH // KVH
    half = KVH * HD
    scale = 1.0 / math.sqrt(HD)
    q_all = query.reshape(reqs, KVH, group, HD)
    keys_c = cache[:, :, :half].reshape(reqs, length, KVH, HD)
    vals_c = cache[:, :, half:].reshape(reqs, length, KVH, HD)
    keys_w = window[:, :half].reshape(-1, KVH, HD)
    vals_w = window[:, half:].reshape(-1, KVH, HD)
    keys_o = own[:, :half].reshape(reqs, KVH, HD)
    vals_o = own[:, half:].astype(jnp.float32).reshape(reqs, KVH, HD)
    s_cache = (
        jnp.einsum("rkgh,rpkh->rkgp", q_all, keys_c, preferred_element_type=jnp.float32) * scale
    )
    places = jnp.arange(length, dtype=jnp.int32)
    s_cache = jnp.where(places[None, None, None, :] < lens[:, None, None, None], s_cache, NEG)
    s_win = jnp.einsum("rkgh,pkh->rkgp", q_all, keys_w, preferred_element_type=jnp.float32) * scale
    rows = jnp.arange(window.shape[0], dtype=jnp.int32)
    live = (rows >= first) & (rows < last)
    leader = jnp.arange(reqs, dtype=jnp.int32) == 0
    usable = leader[:, None] & live[None, :]
    s_win = jnp.where(usable[:, None, None, :], s_win, NEG)
    s_own = jnp.einsum("rkgh,rkh->rkg", q_all, keys_o, preferred_element_type=jnp.float32) * scale
    top = jnp.maximum(jnp.maximum(jnp.max(s_cache, -1), jnp.max(s_win, -1)), s_own)
    e_cache = jnp.exp(s_cache - top[..., None])
    e_win = jnp.exp(s_win - top[..., None])
    e_own = jnp.exp(s_own - top)
    total = jnp.sum(e_cache, -1) + jnp.sum(e_win, -1) + e_own
    p_cache = (e_cache / total[..., None]).astype(jnp.bfloat16)
    p_win = (e_win / total[..., None]).astype(jnp.bfloat16)
    p_own = (e_own / total).astype(jnp.bfloat16).astype(jnp.float32)
    mixed = jnp.einsum("rkgp,rpkh->rkgh", p_cache, vals_c, preferred_element_type=jnp.float32)
    mixed = mixed + jnp.einsum("rkgp,pkh->rkgh", p_win, vals_w, preferred_element_type=jnp.float32)
    mixed = mixed + p_own[..., None] * vals_o[:, :, None, :]
    return mixed.reshape(reqs, QH * HD)


def per_device(
    tokens,
    queries,
    token_kv,
    kv_cache,
    context_lengths,
    fresh_kv,
    block_counts,
    expert_ids,
    route_weights,
    norm_gain,
    w_gate,
    w_up,
    w_down,
):
    me = lax.axis_index(DEV)
    reqs = tokens.shape[0]
    width = tokens.shape[1]
    span = fresh_kv.shape[0]
    following = passed_along(fresh_kv, DEV, -1)
    window = jnp.concatenate([fresh_kv, following], 0)
    offsets = jnp.cumsum(block_counts) - block_counts
    mine = lax.dynamic_index_in_dim(offsets, me, 0, keepdims=False)
    taken = lax.dynamic_index_in_dim(block_counts, me, 0, keepdims=False)
    first = (mine - me * (span // BLOCK)) * BLOCK
    last = first + taken * BLOCK
    attn = attend(queries, kv_cache, context_lengths, token_kv, window, first, last)
    hidden_state = tokens.astype(jnp.float32) + attn
    spread = jnp.mean(hidden_state * hidden_state, -1, keepdims=True)
    normed = (hidden_state * lax.rsqrt(spread + EPS) * norm_gain).astype(jnp.bfloat16)
    labels = jnp.arange(EXPERTS, dtype=jnp.int32)
    coef = jnp.sum(
        route_weights[:, :, None] * (expert_ids[:, :, None] == labels).astype(jnp.float32), 1
    ).reshape(1, 1, reqs * EXPERTS)
    coef = jnp.pad(coef, ((0, 0), (0, 0), (0, 128 - reqs * EXPERTS)))
    stacked = normed.reshape(reqs, 4, 2, width // 8).transpose(2, 1, 0, 3).reshape(2, 4 * reqs, width // 8)
    moe = exchange(stacked, coef, w_gate, w_up, w_down)
    moe = moe.reshape(2, 4, reqs, width // 8).transpose(2, 1, 0, 3).reshape(reqs, width)
    return (hidden_state + moe).astype(jnp.bfloat16)


def solution(mesh):
    split = Mesh(
        mesh.devices.reshape(mesh.shape["groups"], 8, 8, 2), ("groups", "dev_0", "dev_1", "dev_2")
    )
    return jax.shard_map(
        per_device,
        mesh=split,
        in_specs=(
            P(GROUPS_DEV, None),
            P(GROUPS_DEV, None),
            P(GROUPS_DEV, None),
            P(GROUPS_DEV, None, None),
            P(GROUPS_DEV),
            P(GROUPS_DEV, None),
            P("groups"),
            P(GROUPS_DEV, None),
            P(GROUPS_DEV, None),
            P(),
            P(None, DEV),
            P(None, DEV),
            P(DEV, None),
        ),
        out_specs=P(GROUPS_DEV, None),
        check_vma=False,
    )
```

time: 381 us -> 116 us (0.30)
  waiting for transfers between devices: 181 us -> 0.01 us
  Pallas kernels: 0 us -> 87.4 us
  blocking collectives: 53.5 us -> 0 us
  local copies, waits for them, and re-layouts: 53.6 us -> 8.57 us
  matrix products: 30.1 us -> 1.48 us
  other arithmetic: 22.5 us -> 3.63 us
  between operations: 15 us -> 1.57 us
  starting transfers between devices: 23.4 us -> 13.2 us
    all_to_all x1 -> x0, waiting for transfers between devices: 141 us -> none  [turned_blocks(): out = lax.all_to_all(out, axes[k], k, k, tiled=True)]
    pallas_call x0 -> x1, Pallas kernels: none -> 87.4 us  [exchange(): pl.pallas_call(exchange_kernel, out_shape=jax.ShapeDtypeStruct(rows.shape...]
    all_gather x3 -> x0, blocking collectives: 44.8 us -> none  [gather_in_order(): parts = lax.all_gather(parts, axes[k], axis=0, tiled=True)]
    all_gather x1 -> x0, waiting for transfers between devices: 40.3 us -> none  [per_device(): every_row = lax.all_gather(normed, DEV, axis=0, tiled=True)]
    dot_general x4 -> x0, matrix products: 25.9 us -> none  [the longest x1 10.6 us: per_device(): jnp.dot(act, w_down, preferred_element_type=jnp.float32)]
    another operation x3 -> x1, local copies, waits for them, and re-layouts: 18.7 us -> 0.76 us  [the longest x2 17.9 us: turned_blocks(): out = parts.reshape(*(lax.axis_size(a) for a in axes), *inside)]
    reduce_sum x6 -> x1, other arithmetic: 16.9 us -> 0.08 us  [per_device(): jnp.sum(route_weights[:, :, None] * (expert_ids[:, :, None] == labels).as...]
    reshape x3 -> x6, local copies, waits for them, and re-layouts: 13.4 us -> 1.8 us  [the longest x2 1.02 us: per_device(): moe.reshape(2, 4, reqs, width // 8).transpose(2, 1, 0, 3)]
  transfers between devices with their start and end apart: 3 -> 1, of which waited for: 2 -> 0; matrix products, arithmetic and copies ran while one was open for 4% -> 7% of each run, Pallas kernels for 0% -> 0%
where the time goes in v1:
time: 116 us
  Pallas kernels  87.4 us (75%)
  starting transfers between devices  13.2 us (11%)
  local copies, waits for them, and re-layouts  8.57 us (7%)
  other arithmetic  3.63 us (3%)
  between operations  1.57 us (1%)
  matrix products  1.48 us (1%)
    pallas_call x1, Pallas kernels, exchange(): pl.pallas_call(exchange_kernel, out_shape=jax.ShapeDtypeStruct(rows.shape...  87.4 us
    ppermute x1, starting transfers between devices, passed_along(): lax.ppermute(value, axis, [(source, source + steps) for source in range(l...  13.2 us
    unnamed x15, local copies, waits for them, and re-layouts  2.56 us
  transfers between devices with their start and end apart: 1, of which 0 were waited for; matrix products, arithmetic and copies ran while one was open for 7% of the time, Pallas kernels for 0%

profile of v1, /device:TPU:516, one launch (start us, length us, event | category | flops | bytes accessed | tf_op | source)
XLA Modules:
  0.0 115.9 jit_solution(15682279910784239139)
XLA Ops:
  0.0 1.3 %copy.74 = bf16[64,2048]{0,1:T(8,128)(2,1)S(1)} copy(bf16[64,2048]{1,0:T(8,128)(2,1)} %param.18) | data formatting | bytes 524288 | tf_op args[5]
  1.3 13.2 %collective-permute-start = (bf16[64,2048]{0,1:T(8,128)(2,1)S(1)}, bf16[64,2048]{0,1:T(8,128)(2,1)S(1)}, u32[]{:S(2)}, u32[]{:S(2)}) collective-permute-start(bf16[64,2048]{0,1:T(8,128)(2,1)S(1)} %copy.74), channel_id=1, source_target_pairs={{1,0},{2,1},{3,2},{4,3},{5,4},{6,5},{7,6},{8,7},{9,8},{10,9},{11,1... | collective-permute-start | bytes 786440 | tf_op jit(solution)/shard_map/ppermute | solution.py:27
  14.5 0.8 copy.72
  15.3 0.2 reduce-window.9
  15.5 0.7 sub.39
  16.2 1.3 %dynamic_slice.8 = s32[1]{0:T(128)} dynamic-slice(s32[128]{0:T(128)} %param.19, s32[]{:T(128)S(6)} %select_n.57), dynamic_slice_sizes={1} | dynamic-slice | bytes 12 | tf_op jit(solution)/shard_map/jit(dynamic_index_in_dim)/dynamic_slice | solution.py:418
  17.5 0.6 dynamic_slice.7
  19.5 0.9 reshape.177
  20.3 1.3 %slice_bitcast_fusion.1 = (bf16[4,8,8,8,128]{4,3,2,1,0:T(8,128)(2,1)S(1)}, bf16[4,8,8,8,128]{4,3,2,1,0:T(8,128)(2,1)S(1)}) fusion(bf16[4,64,2048]{2,1,0:T(8,128)(2,1)} %param.16), kind=kLoop, calls=%fused_computation.16 | loop fusion | bytes 2097152
  21.7 0.8 fusion.12
  22.5 0.1 fusion.33
  22.9 0.5 pad.4.coef_ref
  23.4 0.5 fusion.31
  23.9 0.3 pad_maximum_fusion
  24.2 0.3 fusion.32
  24.5 0.2 fusion.13
  24.7 0.2 fusion.14
  25.0 0.3 fusion.5
  25.3 0.3 fusion.2
  25.6 0.2 multiply_reduce_fusion
  26.0 0.6 reshape.187.rows_ref
  26.6 87.4 %shard_map.127 = f32[2,16,768]{2,1,0:T(8,128)} custom-call(bf16[2,16,768]{2,1,0:T(8,128)(2,1)} %reshape.187.rows_ref, f32[1,1,128]{2,1,0:T(1,128)} %pad.4.coef_ref, bf16[256,256]{1,0:T(8,128)(2,1)} %get-tuple-element.14.perm_ref, bf16[256,256]{1,0:T(8,128)(2,1)} %get-tuple-element.13.back_ref, bf16[6144,256]{1,0:T(8,128)(2,1)} %gate_hbm.1, ...), custom_call_target="tpu_custom_call" | custom-call | tf_op jit(solution)/shard_map/pallas_call | solution.py:324
  114.1 0.9 reshape.189
  115.2 0.7 add_convert_fusion
  (35 shorter events, 0.9 us)
Async XLA Ops:
  0.0 21.6 %copy-start.5 = (s32[4]{0:T(128)S(1)}, s32[4]{0:T(128)}, u32[]{:S(2)}) copy-start(s32[4]{0:T(128)} %param.17) | copy-start | bytes 52
  0.0 21.7 %copy-start.2 = (bf16[4,2048]{1,0:T(4,128)(2,1)S(1)}, bf16[4,2048]{1,0:T(4,128)(2,1)}, u32[]{:S(2)}) copy-start(bf16[4,2048]{1,0:T(4,128)(2,1)} %param.15) | copy-start | bytes 49156
  0.0 22.7 %copy-start.4 = (s32[4,2]{0,1:T(2,128)S(1)}, s32[4,2]{0,1:T(2,128)}, u32[]{:S(2)}) copy-start(s32[4,2]{0,1:T(2,128)} %param.20) | copy-start | bytes 100
  0.0 22.7 %copy-start.3 = (f32[4,2]{0,1:T(2,128)S(1)}, f32[4,2]{0,1:T(2,128)}, u32[]{:S(2)}) copy-start(f32[4,2]{0,1:T(2,128)} %param.21) | copy-start | bytes 100
  1.3 22.6 %collective-permute-start = (bf16[64,2048]{0,1:T(8,128)(2,1)S(1)}, bf16[64,2048]{0,1:T(8,128)(2,1)S(1)}, u32[]{:S(2)}, u32[]{:S(2)}) collective-permute-start(bf16[64,2048]{0,1:T(8,128)(2,1)S(1)} %copy.74), channel_id=1, source_target_pairs={{1,0},{2,1},{3,2},{4,3},{5,4},{6,5},{7,6},{8,7},{9,8},{10,9},{11,1... | collective-permute-start | bytes 786440 | tf_op jit(solution)/shard_map/ppermute | solution.py:27
  22.5 3.2 %copy-start = (bf16[4,6144]{1,0:T(4,128)(2,1)S(1)}, bf16[4,6144]{1,0:T(4,128)(2,1)}, u32[]{:S(2)}) copy-start(bf16[4,6144]{1,0:T(4,128)(2,1)} %param.13) | copy-start | bytes 147460
  22.5 3.3 %copy-start.1 = (f32[6144]{0:T(1024)S(1)}, f32[6144]{0:T(1024)}, u32[]{:S(2)}) copy-start(f32[6144]{0:T(1024)} %param.22) | copy-start | bytes 73732

commit v2 on v0

v2 whole, which is shorter than its diff:
```python
import math

import jax
import jax.numpy as jnp
from jax import lax
from jax.sharding import Mesh
from jax.sharding import PartitionSpec as P
from jax.experimental import pallas as pl
from jax.experimental.pallas import tpu as pltpu

QH = 48
KVH = 8
HD = 128
EXPERTS = 4
BLOCK = 16
DEV = ("dev_0", "dev_1", "dev_2")
GROUPS_DEV = ("groups", "dev_0", "dev_1", "dev_2")


EPS = 1e-05
NEG = -1e30


MESH_ID = pl.DeviceIdType.MESH
RING = ("dev_1", "dev_0")
LINE = ("dev_0", "dev_1")
OFFSETS = (0, 1, -1, 2, -2, 3, -3, 4)
GROUPS_OF_BLOCKS = ((0, 3), (3, 2), (5, 3))


def slot_at(sign, distance):
    if distance in (0, 4):
        return 2 * distance - distance // 4
    return 2 * distance - (1 + sign) // 2


def slots_of(distance):
    if distance == 0:
        return (0, 1)
    return (2 * distance - 1, 1 if distance == 4 else 2)


def attend(lens_ref, counts_ref, query8, kv_all, me, reqs, span, length):
    sub8 = lax.broadcasted_iota(jnp.int32, (8, HD), 0)
    tiles = []
    for h in range(0, QH, 2):
        a = query8[:, h * HD : (h + 1) * HD]
        b = query8[:, (h + 1) * HD : (h + 2) * HD]
        tiles.append(jnp.where(sub8 < reqs, a, b))
    group = QH // KVH
    rows = group * reqs
    total_keys = kv_all.shape[0]
    half = KVH * HD
    counts = counts_ref[...]
    lane = lax.broadcasted_iota(jnp.int32, counts.shape, 1)
    offset = jnp.sum(jnp.where(lane < me, counts, 0), 1, keepdims=True)
    taken = jnp.sum(jnp.where(lane == me, counts, 0), 1, keepdims=True)
    first = offset * BLOCK - me * span
    stop = first + taken * BLOCK
    key = lax.broadcasted_iota(jnp.int32, (1, total_keys), 1)
    cached = reqs * length
    owner = jnp.full((1, total_keys), -1, jnp.int32)
    for t in range(reqs):
        place = key - t * length
        mine = (place >= 0) & (place < length) & (place < lens_ref[t])
        owner = jnp.where(mine, t, owner)
    place = key - cached
    live = (place >= 0) & (place < 2 * span) & (place >= first) & (place < stop)
    owner = jnp.where(live, 0, owner)
    place = key - (cached + 2 * span)
    owner = jnp.where((place >= 0) & (place < reqs), place, owner)
    row = lax.rem(lax.broadcasted_iota(jnp.int32, (rows, total_keys), 0), reqs)
    valid = row == owner
    mixed = []
    for k in range(KVH):
        q = jnp.concatenate(tiles[k * group // 2 : (k + 1) * group // 2], 0).astype(jnp.bfloat16)
        s = lax.dot_general(
            q,
            kv_all[:, k * HD : (k + 1) * HD],
            (((1,), (1,)), ((), ())),
            preferred_element_type=jnp.float32,
        ) * (1.0 / math.sqrt(HD))
        s = jnp.where(valid, s, NEG)
        e = jnp.exp(s - jnp.max(s, 1, keepdims=True))
        p = (e / jnp.sum(e, 1, keepdims=True)).astype(jnp.bfloat16)
        mixed.append(
            jnp.dot(
                p,
                kv_all[:, half + k * HD : half + (k + 1) * HD],
                preferred_element_type=jnp.float32,
            )
        )
    parts = []
    for k in range(KVH):
        for i in range(group // 2):
            piece = mixed[k][8 * i : 8 * i + 8]
            turned = pltpu.roll(piece, reqs, 0)
            parts.append(jnp.where(sub8 < reqs, piece, turned))
            parts.append(jnp.where(sub8 < reqs, turned, piece))
    return jnp.concatenate(parts, 1)


def layer_kernel(
    lens_ref, ids_ref, route_ref, tokens_ref, queries_ref, own_ref, counts_ref, gain_ref, perm_ref, back_ref,
    cache_hbm, fresh_hbm, gate_hbm, up_hbm, down_hbm, out_ref,
    query8, token8, own8, hidden8, kv_all, coef_row,
    gathered, coefs, coef_cols, wide, sums, act, part, crossed, hops, fin, w_in, w_down,
    sem_w, sem_kv, win_send, win_recv, c_send, c_recv, p_send, p_recv, g_send, g_recv, gx_send, gx_recv,
    x_send, x_recv, r_send, r_recv, f_send, f_recv,
):
    n = lax.axis_size("dev_0")
    half_n = n // 2
    core = lax.axis_index("dev_2")
    other = 1 - core
    sgn = 1 - 2 * core
    xy = {"dev_0": lax.axis_index("dev_0"), "dev_1": lax.axis_index("dev_1")}
    pos = [xy[a] for a in RING]
    line = [xy[a] for a in LINE]
    width = gathered.shape[5]
    reqs = tokens_ref.shape[0]
    length = cache_hbm.shape[1]
    span = fresh_hbm.shape[0]
    devices = 2 * n * n
    me = (xy["dev_0"] * n + xy["dev_1"]) * 2 + core

    def wrap(v):
        return lax.rem(v + 2 * n, n)

    def place_of(index):
        index = lax.rem(index + devices, devices)
        return {"dev_0": index // (2 * n), "dev_1": lax.rem(index // 2, n), "dev_2": lax.rem(index, 2)}

    barrier = pltpu.get_barrier_semaphore()
    for step in (-1, 1):
        pl.semaphore_signal(barrier, inc=1, device_id=place_of(me + step), device_id_type=MESH_ID)
    pl.semaphore_signal(barrier, inc=1, device_id={"dev_2": other}, device_id_type=MESH_ID)
    for axis in LINE:
        for j in range(1, n):
            pl.semaphore_signal(
                barrier, inc=1, device_id={axis: wrap(xy[axis] + j)}, device_id_type=MESH_ID
            )
    kv_loads = [
        pltpu.make_async_copy(cache_hbm.at[t], kv_all.at[pl.ds(t * length, length)], sem_kv.at[t])
        for t in range(reqs)
    ]
    kv_loads.append(
        pltpu.make_async_copy(fresh_hbm, kv_all.at[pl.ds(reqs * length, span)], sem_kv.at[reqs])
    )
    for load in kv_loads:
        load.start()
    quarter = 2 * width
    units = gate_hbm.shape[1]
    loads = []
    for h in range(2):
        for q in range(4):
            for k, src in enumerate((gate_hbm, up_hbm)):
                loads.append(
                    pltpu.make_async_copy(
                        src.at[pl.ds(q * quarter + h * width, width)],
                        w_in.at[h, pl.ds(q * width, width), pl.ds(k * units, units)],
                        sem_w.at[(h * 4 + q) * 2 + k],
                    )
                )
    loads.append(pltpu.make_async_copy(down_hbm, w_down, sem_w.at[16]))
    for load in loads:
        load.start()

    query = queries_ref[...].astype(jnp.float32)
    query8[0:reqs] = query
    query8[reqs : 2 * reqs] = query
    token = tokens_ref[...].astype(jnp.float32)
    token8[0:reqs] = token
    token8[reqs : 2 * reqs] = token
    own8[...] = jnp.zeros_like(own8)
    own8[0:reqs] = own_ref[...].astype(jnp.float32)
    kv_all[pl.ds(reqs * length + 2 * span, 16)] = own8[...].astype(jnp.bfloat16)
    rest = reqs * length + 2 * span + 16
    kv_all[pl.ds(rest, kv_all.shape[0] - rest)] = jnp.zeros(
        (kv_all.shape[0] - rest, kv_all.shape[1]), jnp.bfloat16
    )
    lane = lax.broadcasted_iota(jnp.int32, (1, 128), 1)
    coef = jnp.zeros((1, 128), jnp.float32)
    for t in range(reqs):
        for k in range(2):
            coef = coef + jnp.where(lane == t * EXPERTS + ids_ref[t, k], route_ref[t, k], 0.0)
    coef_row[...] = coef
    pl.semaphore_wait(barrier, 2 * (n - 1) + 3)

    pending = []

    def send(src, dst, s_sem, r_sem, where):
        copy = pltpu.make_async_remote_copy(
            src_ref=src, dst_ref=dst, send_sem=s_sem, recv_sem=r_sem,
            device_id=where, device_id_type=MESH_ID,
        )
        copy.start()
        pending.append(copy)
        return copy

    following = send(
        fresh_hbm, kv_all.at[pl.ds(reqs * length + span, span)], win_send.at[0], win_recv.at[0],
        place_of(me - 1),
    )
    static_slot = {o % n: i for i, o in enumerate(OFFSETS)}
    coefs[core, 0, 0] = coef_row[...]
    coef_firsts = [
        send(
            coef_row, coefs.at[core, 0, static_slot[-j % n]], c_send.at[j], c_recv.at[j],
            {"dev_0": wrap(xy["dev_0"] + j)},
        )
        for j in range(1, n)
    ]
    for load in kv_loads:
        load.wait()
    following.wait_recv()
    hidden = token8[...] + attend(
        lens_ref, counts_ref, query8, kv_all, me, reqs, span, length
    )
    hidden8[...] = hidden
    spread_sq = jnp.mean(hidden * hidden, 1, keepdims=True)
    normed = hidden * lax.rsqrt(spread_sq + EPS) * gain_ref[...]
    sub8 = lax.broadcasted_iota(jnp.int32, (8, 4 * width // 2), 0)
    stacked = jnp.concatenate(
        [
            jnp.where(
                sub8 < reqs,
                normed[:, 2 * i * quarter : (2 * i + 1) * quarter],
                normed[:, (2 * i + 1) * quarter : (2 * i + 2) * quarter],
            )
            for i in range(2)
        ],
        0,
    ).astype(jnp.bfloat16)
    for h in range(2):
        gathered[h, core, 0, 0] = stacked[:, h * width : (h + 1) * width]

    ways = ((0, half_n, sgn), (1, half_n - 1, -sgn))
    passing = {}

    def pass_on(s):
        for h in range(2):
            for way, steps, turn in ways:
                if s > 1 and s - 1 <= steps:
                    passing[h, way, s - 1].wait_recv()
                if s <= steps:
                    passing[h, way, s] = send(
                        gathered.at[h, core, 0, slot_at(-turn, s - 1)],
                        gathered.at[h, core, 0, slot_at(-turn, s)],
                        p_send.at[h, way, s - 1], p_recv.at[h, way, s - 1],
                        {LINE[h]: wrap(line[h] + turn)},
                    )

    rounds = {}
    crossing = {}

    def go_round(s, g):
        low, count = GROUPS_OF_BLOCKS[g]
        at = pl.ds(low, count)
        for h in range(2):
            for way, steps, turn in ways:
                if s > 1 and s - 1 <= steps:
                    rounds[h, way, s - 1, g].wait_recv()
                if s <= steps:
                    rounds[h, way, s, g] = send(
                        gathered.at[h, core, slot_at(-turn, s - 1), at],
                        gathered.at[h, core, slot_at(-turn, s), at],
                        g_send.at[h, way, s - 1, g], g_recv.at[h, way, s - 1, g],
                        {RING[h]: wrap(pos[h] + turn)},
                    )
        for h in range(2):
            first, many = slots_of(s - 1)
            ref = gathered.at[h, core, pl.ds(first, many), at]
            crossing[h, s - 1, g] = send(
                ref, ref, gx_send.at[h, s - 1, g], gx_recv.at[h, s - 1, g], {"dev_2": other}
            )

    batch = 2 * n * reqs
    stack = 4 * batch

    def project(d):
        if d == 0:
            for load in loads[:16]:
                load.wait()
        first, many = slots_of(d)
        for h in range(2):
            for g in range(len(GROUPS_OF_BLOCKS)):
                crossing[h, d, g].wait_recv()
            for i in range(many):
                z = gathered[h, :, first + i].reshape(stack, width)
                z = jnp.dot(perm_ref[...], z, preferred_element_type=jnp.float32).astype(jnp.bfloat16)
                for q in range(4):
                    wide[i * batch : (i + 1) * batch, q * width : (q + 1) * width] = z[
                        q * batch : (q + 1) * batch
                    ]
            sums[h, first * batch : (first + many) * batch] = jnp.dot(
                wide[0 : many * batch], w_in[h], preferred_element_type=jnp.float32
            )

    pass_on(1)
    pass_on(2)
    go_round(1, 0)
    for copy in coef_firsts:
        copy.wait_recv()
    coef_seconds = [
        send(
            coefs.at[core, 0], coefs.at[core, static_slot[-j % n]],
            c_send.at[n + j], c_recv.at[n + j], {"dev_1": wrap(xy["dev_1"] + j)},
        )
        for j in range(1, n)
    ]
    pass_on(3)
    go_round(1, 1)
    pass_on(4)
    go_round(2, 0)
    pass_on(5)
    go_round(1, 2)
    for copy in coef_seconds:
        copy.wait_recv()
    coef_both = send(coefs.at[core], coefs.at[core], c_send.at[0], c_recv.at[0], {"dev_2": other})
    go_round(2, 1)
    go_round(3, 0)
    project(0)
    go_round(2, 2)
    go_round(3, 1)
    go_round(4, 0)
    coef_both.wait_recv()
    expert = me // (devices // EXPERTS)
    row8 = lax.broadcasted_iota(jnp.int32, (8, 128), 0)
    lane8 = lax.broadcasted_iota(jnp.int32, (8, 128), 1)
    keep = lane8 == lax.rem(row8, reqs) * EXPERTS + expert
    for r in range(n):
        for c in range(n):
            both = jnp.where(row8 < reqs, coefs[0, r, c], coefs[1, r, c])
            coef_cols[r, c] = jnp.broadcast_to(
                jnp.sum(jnp.where(keep, both, 0.0), 1, keepdims=True), (8, 128)
            )
    project(1)
    go_round(3, 2)
    go_round(4, 1)
    project(2)
    go_round(4, 2)
    go_round(5, 0)
    go_round(5, 1)
    project(3)
    go_round(5, 2)
    project(4)

    for r in range(n):
        both = sums[0, r * batch : (r + 1) * batch] + jnp.concatenate(
            [sums[1, c * batch + r * 8 : c * batch + (r + 1) * 8] for c in range(n)], 0
        )
        gate = both[:, :units]
        up = both[:, units:]
        coef = coef_cols[r].reshape(batch, 128)
        coef = jnp.concatenate([coef] * (units // 128), 1)
        act[r] = (gate / (1.0 + jnp.exp(-gate)) * up * coef).reshape(n, 8, units)
    loads[16].wait()

    crossed_copies = {}

    def descend(d):
        first, many = slots_of(d)
        for h in range(2):
            if h == 0:
                rows = [act[first + i].reshape(batch, units) for i in range(many)]
            else:
                rows = [act[:, first + i].reshape(batch, units) for i in range(many)]
            a = jnp.concatenate(rows, 0).astype(jnp.bfloat16)
            for q in range(4):
                wide[0 : many * batch, q * width : (q + 1) * width] = jnp.dot(
                    a,
                    w_down[:, q * quarter + h * width : q * quarter + (h + 1) * width],
                    preferred_element_type=jnp.float32,
                ).astype(jnp.bfloat16)
            for i in range(many):
                z = jnp.concatenate(
                    [
                        wide[i * batch : (i + 1) * batch, q * width : (q + 1) * width]
                        for q in range(4)
                    ],
                    0,
                )
                z = jnp.dot(back_ref[...], z, preferred_element_type=jnp.float32)
                part[h, :, first + i] = z.astype(jnp.bfloat16).reshape(2, n, 16, width)
            at = pl.ds(first, many)
            crossed_copies[h, d] = send(
                part.at[h, other, at], crossed.at[h, at], x_send.at[h, d], x_recv.at[h, d],
                {"dev_2": other},
            )

    held = {}

    def collect(k):
        distance = half_n + 1 - k
        for h in range(2):
            crossed_copies[h, distance].wait_recv()
        for g in (2, 1, 0):
            low, count = GROUPS_OF_BLOCKS[g]
            at = pl.ds(low, count)
            for h in range(2):
                for way, steps, turn in ways:
                    s = k - (half_n - steps)
                    if s < 1:
                        continue
                    slot = slot_at(turn, distance)
                    total = part[h, core, slot, at].astype(jnp.float32) + crossed[h, slot, at].astype(
                        jnp.float32
                    )
                    if s > 1:
                        held[h, way, s - 1, g].wait_recv()
                        total = total + hops[h, way, s - 2, at].astype(jnp.float32)
                    part[h, core, slot, at] = total.astype(jnp.bfloat16)
                    held[h, way, s, g] = send(
                        part.at[h, core, slot, at], hops.at[h, way, s - 1, at],
                        r_send.at[h, way, s - 1, g], r_recv.at[h, way, s - 1, g],
                        {RING[h]: wrap(pos[h] + turn)},
                    )

    def collect_own(g):
        low, count = GROUPS_OF_BLOCKS[g]
        at = pl.ds(low, count)
        for h in range(2):
            total = part[h, core, 0, at].astype(jnp.float32) + crossed[h, 0, at].astype(jnp.float32)
            for way, steps, turn in ways:
                held[h, way, steps, g].wait_recv()
                total = total + hops[h, way, steps - 1, at].astype(jnp.float32)
            part[h, core, 0, at] = total.astype(jnp.bfloat16)

    finals = {}

    def finish(k):
        distance = half_n + 1 - k
        for h in range(2):
            for way, steps, turn in ways:
                s = k - (half_n - steps)
                if s < 1:
                    continue
                slot = slot_at(turn, distance)
                if s > 1:
                    finals[h, way, s - 1].wait_recv()
                    part[h, core, 0, slot] = (
                        part[h, core, 0, slot].astype(jnp.float32)
                        + fin[h, way, s - 2].astype(jnp.float32)
                    ).astype(jnp.bfloat16)
                finals[h, way, s] = send(
                    part.at[h, core, 0, slot], fin.at[h, way, s - 1],
                    f_send.at[h, way, s - 1], f_recv.at[h, way, s - 1],
                    {LINE[h]: wrap(line[h] + turn)},
                )

    descend(4)
    descend(3)
    collect(1)
    descend(2)
    collect(2)
    descend(1)
    collect(3)
    descend(0)
    collect(4)
    for h in range(2):
        crossed_copies[h, 0].wait_recv()
    collect_own(2)
    finish(1)
    collect_own(1)
    finish(2)
    collect_own(0)
    finish(3)
    finish(4)
    totals = []
    for h in range(2):
        total = part[h, core, 0, 0].astype(jnp.float32)
        for way, steps, turn in ways:
            finals[h, way, steps].wait_recv()
            total = total + fin[h, way, steps - 1].astype(jnp.float32)
        totals.append(total)
    moe = jnp.concatenate(totals, 1)
    pieces = []
    for i in range(2):
        pieces.append(moe[8 * i : 8 * i + 8])
        pieces.append(pltpu.roll(moe[8 * i : 8 * i + 8], reqs, 0))
    final = hidden8[...] + jnp.concatenate(pieces, 1)
    out_ref[...] = final[0:reqs].astype(jnp.bfloat16)
    for copy in pending:
        copy.wait_send()


def per_device(
    tokens,
    queries,
    token_kv,
    kv_cache,
    context_lengths,
    fresh_kv,
    block_counts,
    expert_ids,
    route_weights,
    norm_gain,
    w_gate,
    w_up,
    w_down,
):
    n = lax.axis_size("dev_0")
    reqs, full = tokens.shape
    width = full // 8
    units = w_gate.shape[1]
    rows = 2 * n * n * reqs
    size = 4 * 2 * n * reqs
    r = jnp.arange(size, dtype=jnp.int32)
    q, b, c, t = r // (size // 4), (r // (2 * reqs)) % n, (r // reqs) % 2, r % reqs
    source = c * (size // 2) + b * 16 + q * reqs + t
    perm = (source[:, None] == r[None, :]).astype(jnp.bfloat16)
    back = perm.T
    vmem = pl.BlockSpec(memory_space=pltpu.VMEM)
    smem = pl.BlockSpec(memory_space=pltpu.SMEM)
    anyspace = pl.BlockSpec(memory_space=pl.ANY)
    bf = jnp.bfloat16
    f32 = jnp.float32
    dma = pltpu.SemaphoreType.DMA
    half_n = n // 2
    keys = reqs * kv_cache.shape[1] + 2 * fresh_kv.shape[0] + 128
    return pl.pallas_call(
        layer_kernel,
        out_shape=jax.ShapeDtypeStruct(tokens.shape, bf),
        in_specs=[smem] * 3 + [vmem] * 7 + [anyspace] * 5,
        out_specs=vmem,
        scratch_shapes=[
            pltpu.VMEM((2 * reqs, full), f32),
            pltpu.VMEM((2 * reqs, full), f32),
            pltpu.VMEM((16, token_kv.shape[1]), f32),
            pltpu.VMEM((2 * reqs, full), f32),
            pltpu.VMEM((keys, token_kv.shape[1]), bf),
            pltpu.VMEM((1, 128), f32),
            pltpu.VMEM((2, 2, n, n, 16, width), bf),
            pltpu.VMEM((2, n, n, 1, 128), f32),
            pltpu.VMEM((n, n, 8, 128), f32),
            pltpu.VMEM((4 * n * reqs, full // 2), bf),
            pltpu.VMEM((2, rows, 2 * units), f32),
            pltpu.VMEM((n, n, 8, units), f32),
            pltpu.VMEM((2, 2, n, n, 16, width), bf),
            pltpu.VMEM((2, n, n, 16, width), bf),
            pltpu.VMEM((2, 2, half_n, n, 16, width), bf),
            pltpu.VMEM((2, 2, half_n, 16, width), bf),
            pltpu.VMEM((2, full // 2, 2 * units), bf),
            pltpu.VMEM(w_down.shape, bf),
            dma((17,)),
            dma((reqs + 1,)),
            dma((1,)), dma((1,)),
            dma((2 * n,)), dma((2 * n,)),
            dma((2, 2, half_n)), dma((2, 2, half_n)),
            dma((2, 2, half_n, 3)), dma((2, 2, half_n, 3)),
            dma((2, half_n + 1, 3)), dma((2, half_n + 1, 3)),
            dma((2, half_n + 1)), dma((2, half_n + 1)),
            dma((2, 2, half_n, 3)), dma((2, 2, half_n, 3)),
            dma((2, 2, half_n)), dma((2, 2, half_n)),
        ],
        compiler_params=pltpu.CompilerParams(
            collective_id=0, has_side_effects=True, vmem_limit_bytes=60 * 1024 * 1024
        ),
    )(
        context_lengths, expert_ids, route_weights, tokens, queries, token_kv,
        block_counts.reshape(1, -1), norm_gain.reshape(1, -1), perm, back,
        kv_cache, fresh_kv, w_gate, w_up, w_down,
    )


def solution(mesh):
    split = Mesh(
        mesh.devices.reshape(mesh.shape["groups"], 8, 8, 2), ("groups", "dev_0", "dev_1", "dev_2")
    )
    return jax.shard_map(
        per_device,
        mesh=split,
        in_specs=(
            P(GROUPS_DEV, None),
            P(GROUPS_DEV, None),
            P(GROUPS_DEV, None),
            P(GROUPS_DEV, None, None),
            P(GROUPS_DEV),
            P(GROUPS_DEV, None),
            P("groups"),
            P(GROUPS_DEV, None),
            P(GROUPS_DEV, None),
            P(),
            P(None, DEV),
            P(None, DEV),
            P(DEV, None),
        ),
        out_specs=P(GROUPS_DEV, None),
        check_vma=False,
    )
```

time: 381 us -> 102 us (0.27)
  waiting for transfers between devices: 181 us -> 0 us
  Pallas kernels: 0 us -> 96.9 us
  blocking collectives: 53.5 us -> 0 us
  local copies, waits for them, and re-layouts: 53.6 us -> 4.12 us
  matrix products: 30.1 us -> 0 us
  starting transfers between devices: 23.4 us -> 0 us
  other arithmetic: 22.5 us -> 0.76 us
  between operations: 15 us -> 0.01 us
    all_to_all x1 -> x0, waiting for transfers between devices: 141 us -> none  [turned_blocks(): out = lax.all_to_all(out, axes[k], k, k, tiled=True)]
    pallas_call x0 -> x1, Pallas kernels: none -> 96.9 us  [per_device(): pl.pallas_call(layer_kernel, out_shape=jax.ShapeDtypeStruct(tokens.shape,...]
    all_gather x3 -> x0, blocking collectives: 44.8 us -> none  [gather_in_order(): parts = lax.all_gather(parts, axes[k], axis=0, tiled=True)]
    all_gather x1 -> x0, waiting for transfers between devices: 40.3 us -> none  [per_device(): every_row = lax.all_gather(normed, DEV, axis=0, tiled=True)]
    dot_general x9 -> x0, matrix products: 30.1 us -> none  [the longest x1 10.6 us: per_device(): jnp.dot(act, w_down, preferred_element_type=jnp.float32)]
    another operation x3 -> x0, local copies, waits for them, and re-layouts: 18.7 us -> none  [the longest x2 17.9 us: turned_blocks(): out = parts.reshape(*(lax.axis_size(a) for a in axes), *inside)]
    reduce_sum x9 -> x0, other arithmetic: 17.5 us -> none  [the longest x2 16.8 us: per_device(): jnp.sum(exchange_by_chip(part.reshape(sources, items, cols), (('dev_0', '...]
    reshape x6 -> x0, local copies, waits for them, and re-layouts: 15.2 us -> none  [the longest x1 12.3 us: per_device(): rows = arrived.reshape(sources * items, cols)]
  transfers between devices with their start and end apart: 3 -> 0, of which waited for: 2 -> 0; matrix products, arithmetic and copies ran while one was open for 4% -> 0% of each run, Pallas kernels for 0% -> 0%
where the time goes in v2:
time: 102 us
  Pallas kernels  96.9 us (95%)
  local copies, waits for them, and re-layouts  4.12 us (4%)
    pallas_call x1, Pallas kernels, per_device(): pl.pallas_call(layer_kernel, out_shape=jax.ShapeDtypeStruct(tokens.shape,...  96.9 us
    unnamed x3, local copies, waits for them, and re-layouts  4.12 us

profile of v2, /device:TPU:516, one launch (start us, length us, event | category | flops | bytes accessed | tf_op | source)
XLA Modules:
  0.0 101.8 jit_solution(3813223100645802400)
XLA Ops:
  0.0 1.3 %copy.14.ids_ref = s32[4,2]{1,0:T(4,128)} copy(s32[4,2]{0,1:T(2,128)} %param.20) | data formatting | bytes 64 | tf_op args[7]
  1.3 1.3 %copy.15.route_ref = f32[4,2]{1,0:T(4,128)} copy(f32[4,2]{0,1:T(2,128)} %param.21) | data formatting | bytes 64 | tf_op args[8]
  2.7 0.8 fusion.1
  3.4 96.9 %shard_map.127 = bf16[4,6144]{1,0:T(4,128)(2,1)} custom-call(s32[4]{0:T(128)} %lens_ref.1, s32[4,2]{1,0:T(4,128)} %copy.14.ids_ref, f32[4,2]{1,0:T(4,128)} %copy.15.route_ref, bf16[4,6144]{1,0:T(4,128)(2,1)} %tokens_ref.1, bf16[4,6144]{1,0:T(4,128)(2,1)} %queries_ref.1, bf16[4,2048]{1,0:T(4,128)(2,1)} %own_ref.1, s32[1,128]{1,0:T(1,128)} %bitcast.3, ...), custom_call_target="tpu_custom_call" | custom-call | tf_op jit(solution)/shard_map/pallas_call | solution.py:521
  100.3 1.4 %copy.17 = bf16[4,6144]{1,0:T(4,128)(2,1)} copy(bf16[4,6144]{1,0:T(4,128)(2,1)} %shard_map.127) | data formatting | bytes 98304
  (1 shorter events, 0.0 us)

commit v3 on v2

v3 whole, which is shorter than its diff:
```python
import math

import jax
import jax.numpy as jnp
from jax import lax
from jax.sharding import Mesh
from jax.sharding import PartitionSpec as P
from jax.experimental import pallas as pl
from jax.experimental.pallas import tpu as pltpu

QH = 48
KVH = 8
HD = 128
EXPERTS = 4
BLOCK = 16
DEV = ("dev_0", "dev_1", "dev_2")
GROUPS_DEV = ("groups", "dev_0", "dev_1", "dev_2")


EPS = 1e-05
NEG = -1e30


MESH_ID = pl.DeviceIdType.MESH
RING = ("dev_1", "dev_0")
LINE = ("dev_0", "dev_1")
OFFSETS = (0, 1, -1, 2, -2, 3, -3, 4)
GROUPS_OF_BLOCKS = ((0, 3), (3, 2), (5, 3))
NEAR_AND_FAR = ((0, 5), (5, 3))


def slot_at(sign, distance):
    if distance in (0, 4):
        return 2 * distance - distance // 4
    return 2 * distance - (1 + sign) // 2


def slots_of(distance):
    if distance == 0:
        return (0, 1)
    return (2 * distance - 1, 1 if distance == 4 else 2)


def query_rows(query8, reqs):
    sub8 = lax.broadcasted_iota(jnp.int32, (8, HD), 0)
    group = QH // KVH
    tiles = []
    for h in range(0, QH, 2):
        a = query8[:, h * HD : (h + 1) * HD]
        b = query8[:, (h + 1) * HD : (h + 2) * HD]
        tiles.append(jnp.where(sub8 < reqs, a, b))
    return [
        jnp.concatenate(tiles[k * group // 2 : (k + 1) * group // 2], 0).astype(jnp.bfloat16)
        for k in range(KVH)
    ]


def scores_of(q, keys):
    return lax.dot_general(
        q, keys, (((1,), (1,)), ((), ())), preferred_element_type=jnp.float32
    ) * (1.0 / math.sqrt(HD))


def attend_held(lens_ref, queries, kv_all, reqs, length, held):
    half = KVH * HD
    rows = queries[0].shape[0]
    key = lax.broadcasted_iota(jnp.int32, (1, held), 1)
    owner = jnp.full((1, held), -1, jnp.int32)
    for t in range(reqs):
        place = key - t * length
        mine = (place >= 0) & (place < length) & (place < lens_ref[0:1, t : t + 1])
        owner = jnp.where(mine, t, owner)
    place = key - reqs * length
    owner = jnp.where((place >= 0) & (place < reqs), place, owner)
    row = lax.rem(lax.broadcasted_iota(jnp.int32, (rows, held), 0), reqs)
    valid = row == owner
    states = []
    for k in range(KVH):
        s = scores_of(queries[k], kv_all[0:held, k * HD : (k + 1) * HD])
        s = jnp.where(valid, s, NEG)
        top = jnp.max(s, 1, keepdims=True)
        e = jnp.exp(s - top)
        total = jnp.sum(e, 1, keepdims=True)
        mixed = jnp.dot(
            e.astype(jnp.bfloat16),
            kv_all[0:held, half + k * HD : half + (k + 1) * HD],
            preferred_element_type=jnp.float32,
        )
        states.append((top, total, mixed))
    return states


def heads_aside(mixed, reqs):
    sub8 = lax.broadcasted_iota(jnp.int32, (8, HD), 0)
    parts = []
    for piece_of in mixed:
        for i in range(QH // KVH // 2):
            piece = piece_of[8 * i : 8 * i + 8]
            turned = pltpu.roll(piece, reqs, 0)
            parts.append(jnp.where(sub8 < reqs, piece, turned))
            parts.append(jnp.where(sub8 < reqs, turned, piece))
    return jnp.concatenate(parts, 1)


def attend_window(counts_ref, queries, states, kv_all, me, reqs, span, held):
    half = KVH * HD
    rows = queries[0].shape[0]
    counts = counts_ref[...]
    lane = lax.broadcasted_iota(jnp.int32, counts.shape, 1)
    offset = jnp.sum(jnp.where(lane < me, counts, 0), 1, keepdims=True)
    taken = jnp.sum(jnp.where(lane == me, counts, 0), 1, keepdims=True)
    first = offset * BLOCK - me * span
    stop = first + taken * BLOCK
    place = lax.broadcasted_iota(jnp.int32, (rows, 2 * span), 1)
    row = lax.rem(lax.broadcasted_iota(jnp.int32, (rows, 2 * span), 0), reqs)
    live = (row == 0) & (place >= first) & (place < stop)
    parts = []
    for k in range(KVH):
        top, total, mixed = states[k]
        s = scores_of(queries[k], kv_all[held : held + 2 * span, k * HD : (k + 1) * HD])
        s = jnp.where(live, s, NEG)
        new = jnp.maximum(top, jnp.max(s, 1, keepdims=True))
        fade = jnp.exp(top - new)
        e = jnp.exp(s - new)
        total = total * fade + jnp.sum(e, 1, keepdims=True)
        mixed = mixed * fade + jnp.dot(
            e.astype(jnp.bfloat16),
            kv_all[held : held + 2 * span, half + k * HD : half + (k + 1) * HD],
            preferred_element_type=jnp.float32,
        )
        parts.append(mixed / total)
    return heads_aside(parts, reqs)


def layer_kernel(
    lens_hbm, ids_hbm, route_hbm, tokens_hbm, queries_hbm, own_hbm, counts_hbm, gain_hbm,
    cache_hbm, fresh_hbm, gate_hbm, up_hbm, down_hbm, out_ref,
    lens_ref, ids_ref, route_ref, tokens_ref, queries_ref, own_ref, counts_ref, gain_ref,
    query8, token8, own8, hidden8, kv_all, coef_row, perm_ref, back_ref,
    gathered, coefs, coef_cols, wide, sums, act, part, crossed, hops, fin, w_in, w_down,
    sem_w, sem_kv, sem_in, win_send, win_recv, c_send, c_recv, p_send, p_recv, g_send, g_recv, gx_send, gx_recv,
    x_send, x_recv, r_send, r_recv, f_send, f_recv,
):
    n = lax.axis_size("dev_0")
    half_n = n // 2
    core = lax.axis_index("dev_2")
    other = 1 - core
    sgn = 1 - 2 * core
    xy = {"dev_0": lax.axis_index("dev_0"), "dev_1": lax.axis_index("dev_1")}
    pos = [xy[a] for a in RING]
    line = [xy[a] for a in LINE]
    width = gathered.shape[6]
    reqs = tokens_hbm.shape[0]
    length = cache_hbm.shape[1]
    span = fresh_hbm.shape[0]
    devices = 2 * n * n
    held = reqs * length + 128
    me = (xy["dev_0"] * n + xy["dev_1"]) * 2 + core

    def wrap(v):
        return lax.rem(v + 2 * n, n)

    def place_of(index):
        index = lax.rem(index + devices, devices)
        return {"dev_0": index // (2 * n), "dev_1": lax.rem(index // 2, n), "dev_2": lax.rem(index, 2)}

    barrier = pltpu.get_barrier_semaphore()
    for step in (-1, 1):
        pl.semaphore_signal(barrier, inc=1, device_id=place_of(me + step), device_id_type=MESH_ID)
    pl.semaphore_signal(barrier, inc=1, device_id={"dev_2": other}, device_id_type=MESH_ID)
    for axis in LINE:
        for j in range(1, n):
            pl.semaphore_signal(
                barrier, inc=1, device_id={axis: wrap(xy[axis] + j)}, device_id_type=MESH_ID
            )
    kv_loads = [
        pltpu.make_async_copy(cache_hbm.at[t], kv_all.at[pl.ds(t * length, length)], sem_kv.at[t])
        for t in range(reqs)
    ]
    kv_loads.append(
        pltpu.make_async_copy(fresh_hbm, kv_all.at[pl.ds(held, span)], sem_kv.at[reqs])
    )
    small = (
        (queries_hbm, queries_ref), (tokens_hbm, tokens_ref), (own_hbm, own_ref), (lens_hbm, lens_ref),
        (ids_hbm, ids_ref), (route_hbm, route_ref), (counts_hbm, counts_ref), (gain_hbm, gain_ref),
    )
    small_loads = [
        pltpu.make_async_copy(src, dst, sem_in.at[i]) for i, (src, dst) in enumerate(small)
    ]
    for load in small_loads + kv_loads:
        load.start()
    quarter = 2 * width
    units = gate_hbm.shape[1]
    loads = []
    for h in range(2):
        for q in range(4):
            for k, src in enumerate((gate_hbm, up_hbm)):
                loads.append(
                    pltpu.make_async_copy(
                        src.at[pl.ds(q * quarter + h * width, width)],
                        w_in.at[h, pl.ds(q * width, width), pl.ds(k * units, units)],
                        sem_w.at[(h * 4 + q) * 2 + k],
                    )
                )
    loads.append(pltpu.make_async_copy(down_hbm, w_down, sem_w.at[16]))
    for load in loads:
        load.start()

    for load in small_loads:
        load.wait()
    query = queries_ref[...].astype(jnp.float32)
    query8[0:reqs] = query
    query8[reqs : 2 * reqs] = query
    token = tokens_ref[...].astype(jnp.float32)
    token8[0:reqs] = token
    token8[reqs : 2 * reqs] = token
    own8[...] = jnp.zeros_like(own8)
    own8[0:reqs] = own_ref[...].astype(jnp.float32)
    kv_all[pl.ds(reqs * length, 16)] = own8[...].astype(jnp.bfloat16)
    kv_all[pl.ds(reqs * length + 16, 112)] = jnp.zeros((112, kv_all.shape[1]), jnp.bfloat16)
    lane = lax.broadcasted_iota(jnp.int32, (1, 128), 1)
    coef = jnp.zeros((1, 128), jnp.float32)
    for t in range(reqs):
        for k in range(2):
            coef = coef + jnp.where(lane == t * EXPERTS + ids_ref[k : k + 1, t : t + 1], route_ref[k : k + 1, t : t + 1], 0.0)
    coef_row[...] = coef
    kv_loads[reqs].wait()
    pl.semaphore_wait(barrier, 2 * (n - 1) + 3)

    pending = []

    def send(src, dst, s_sem, r_sem, where):
        copy = pltpu.make_async_remote_copy(
            src_ref=src, dst_ref=dst, send_sem=s_sem, recv_sem=r_sem,
            device_id=where, device_id_type=MESH_ID,
        )
        copy.start()
        pending.append(copy)
        return copy

    following = send(
        kv_all.at[pl.ds(held, span)], kv_all.at[pl.ds(held + span, span)], win_send.at[0], win_recv.at[0],
        place_of(me - 1),
    )
    static_slot = {o % n: i for i, o in enumerate(OFFSETS)}
    coefs[core, 0, 0] = coef_row[...]
    coef_firsts = [
        send(
            coef_row, coefs.at[core, 0, static_slot[-j % n]], c_send.at[j], c_recv.at[j],
            {"dev_0": wrap(xy["dev_0"] + j)},
        )
        for j in range(1, n)
    ]
    size = perm_ref.shape[0]

    def parts_of(r):
        return r // (size // 4), lax.rem(r // (2 * reqs), n), lax.rem(r // reqs, 2), lax.rem(r, reqs)

    def stacked_row(r):
        q, b, c, t = parts_of(r)
        return c * (size // 2) + b * 16 + q * reqs + t

    def waved_row(r):
        q, b, c, t = parts_of(r)
        wave = 1 - t // 2
        return wave * (size // 2) + c * (size // 4) + b * 8 + lax.rem(t, 2) * 4 + q

    row = lax.broadcasted_iota(jnp.int32, (size, 1), 0)
    column = lax.broadcasted_iota(jnp.int32, (1, size), 1)
    perm_ref[...] = (waved_row(row) == column).astype(jnp.float32).astype(jnp.bfloat16)
    back_ref[...] = (row == stacked_row(column)).astype(jnp.float32).astype(jnp.bfloat16)
    for load in kv_loads[:reqs]:
        load.wait()
    queries = query_rows(query8, reqs)
    states = attend_held(lens_ref, queries, kv_all, reqs, length, held)
    token = token8[...]
    gain = gain_ref[...]
    row8 = lax.broadcasted_iota(jnp.int32, (8, quarter), 0)

    def normed_of(hidden):
        mean = jnp.mean(hidden * hidden, 1, keepdims=True)
        return hidden * lax.rsqrt(mean + EPS) * gain

    def put(wave, normed):
        block = jnp.zeros((8, quarter), jnp.float32)
        for i in range(2):
            t = 2 * (1 - wave) + i
            for q in range(4):
                line_of = jnp.broadcast_to(
                    normed[t : t + 1, q * quarter : (q + 1) * quarter], (8, quarter)
                )
                block = jnp.where(row8 == i * 4 + q, line_of, block)
        block = block.astype(jnp.bfloat16)
        for h in range(2):
            gathered[wave, h, core, 0, 0] = block[:, h * width : (h + 1) * width]

    passing = {}

    def depart(wave):
        for slot in range(1, n):
            for h in range(2):
                offset = OFFSETS[slot]
                passing[wave, h, slot] = send(
                    gathered.at[wave, h, core, 0, 0],
                    gathered.at[wave, h, core, 0, static_slot[-offset % n]],
                    p_send.at[wave, h, slot], p_recv.at[wave, h, slot],
                    {LINE[h]: wrap(line[h] + offset)},
                )

    early = heads_aside([mixed / total for _, total, mixed in states], reqs)
    put(0, normed_of(token + early))
    depart(0)
    following.wait_recv()
    hidden = token + attend_window(
        counts_ref, queries, states, kv_all, me, reqs, span, held
    )
    hidden8[...] = hidden
    put(1, normed_of(hidden))
    depart(1)

    ways = ((0, half_n, sgn), (1, half_n - 1, -sgn))
    def arrive(wave, g):
        low, count = NEAR_AND_FAR[g]
        for slot in range(max(low, 1), low + count):
            for h in range(2):
                passing[wave, h, slot].wait_recv()

    rounds = {}
    crossing = {}

    def go_round(wave, s, g):
        low, count = NEAR_AND_FAR[g]
        at = pl.ds(low, count)
        for h in range(2):
            for way, steps, turn in ways:
                if s > 1 and s - 1 <= steps:
                    rounds[wave, h, way, s - 1, g].wait_recv()
                if s <= steps:
                    rounds[wave, h, way, s, g] = send(
                        gathered.at[wave, h, core, slot_at(-turn, s - 1), at],
                        gathered.at[wave, h, core, slot_at(-turn, s), at],
                        g_send.at[wave, h, way, s - 1, g], g_recv.at[wave, h, way, s - 1, g],
                        {RING[h]: wrap(pos[h] + turn)},
                    )
        for h in range(2):
            first, many = slots_of(s - 1)
            ref = gathered.at[wave, h, core, pl.ds(first, many), at]
            crossing[wave, h, s - 1, g] = send(
                ref, ref, gx_send.at[wave, h, s - 1, g], gx_recv.at[wave, h, s - 1, g],
                {"dev_2": other},
            )

    batch = 2 * n * reqs
    stack = 4 * batch

    def project(d):
        if d == 0:
            for load in loads[:16]:
                load.wait()
        first, many = slots_of(d)
        for h in range(2):
            for wave in range(2):
                for g in range(len(NEAR_AND_FAR)):
                    crossing[wave, h, d, g].wait_recv()
            for i in range(many):
                z = gathered[:, h, :, first + i].reshape(stack, width)
                z = jnp.dot(perm_ref[...], z, preferred_element_type=jnp.float32).astype(jnp.bfloat16)
                for q in range(4):
                    wide[i * batch : (i + 1) * batch, q * width : (q + 1) * width] = z[
                        q * batch : (q + 1) * batch
                    ]
            sums[h, first * batch : (first + many) * batch] = jnp.dot(
                wide[0 : many * batch], w_in[h], preferred_element_type=jnp.float32
            )

    arrive(0, 0)
    go_round(0, 1, 0)
    arrive(0, 1)
    go_round(0, 1, 1)
    for copy in coef_firsts:
        copy.wait_recv()
    coef_seconds = [
        send(
            coefs.at[core, 0], coefs.at[core, static_slot[-j % n]],
            c_send.at[n + j], c_recv.at[n + j], {"dev_1": wrap(xy["dev_1"] + j)},
        )
        for j in range(1, n)
    ]
    go_round(0, 2, 0)
    arrive(1, 0)
    go_round(1, 1, 0)
    go_round(0, 2, 1)
    arrive(1, 1)
    go_round(1, 1, 1)
    for copy in coef_seconds:
        copy.wait_recv()
    coef_both = send(coefs.at[core], coefs.at[core], c_send.at[0], c_recv.at[0], {"dev_2": other})
    go_round(0, 3, 0)
    go_round(1, 2, 0)
    project(0)
    go_round(0, 3, 1)
    go_round(1, 2, 1)
    go_round(0, 4, 0)
    go_round(1, 3, 0)
    coef_both.wait_recv()
    expert = me // (devices // EXPERTS)
    row8 = lax.broadcasted_iota(jnp.int32, (8, 128), 0)
    lane8 = lax.broadcasted_iota(jnp.int32, (8, 128), 1)
    keep = lane8 == lax.rem(row8, reqs) * EXPERTS + expert
    for r in range(n):
        for c in range(n):
            both = jnp.where(row8 < reqs, coefs[0, r, c], coefs[1, r, c])
            coef_cols[r, c] = jnp.broadcast_to(
                jnp.sum(jnp.where(keep, both, 0.0), 1, keepdims=True), (8, 128)
            )
    project(1)
    go_round(0, 4, 1)
    go_round(1, 3, 1)
    go_round(0, 5, 0)
    go_round(1, 4, 0)
    project(2)
    go_round(0, 5, 1)
    go_round(1, 4, 1)
    go_round(1, 5, 0)
    project(3)
    go_round(1, 5, 1)
    project(4)

    for r in range(n):
        both = sums[0, r * batch : (r + 1) * batch] + jnp.concatenate(
            [sums[1, c * batch + r * 8 : c * batch + (r + 1) * 8] for c in range(n)], 0
        )
        gate = both[:, :units]
        up = both[:, units:]
        coef = coef_cols[r].reshape(batch, 128)
        coef = jnp.concatenate([coef] * (units // 128), 1)
        act[r] = (gate / (1.0 + jnp.exp(-gate)) * up * coef).reshape(n, 8, units)
    loads[16].wait()

    crossed_copies = {}

    def descend(d):
        first, many = slots_of(d)
        for h in range(2):
            if h == 0:
                rows = [act[first + i].reshape(batch, units) for i in range(many)]
            else:
                rows = [act[:, first + i].reshape(batch, units) for i in range(many)]
            a = jnp.concatenate(rows, 0).astype(jnp.bfloat16)
            for q in range(4):
                wide[0 : many * batch, q * width : (q + 1) * width] = jnp.dot(
                    a,
                    w_down[:, q * quarter + h * width : q * quarter + (h + 1) * width],
                    preferred_element_type=jnp.float32,
                ).astype(jnp.bfloat16)
            for i in range(many):
                z = jnp.concatenate(
                    [
                        wide[i * batch : (i + 1) * batch, q * width : (q + 1) * width]
                        for q in range(4)
                    ],
                    0,
                )
                z = jnp.dot(back_ref[...], z, preferred_element_type=jnp.float32)
                part[h, :, first + i] = z.astype(jnp.bfloat16).reshape(2, n, 16, width)
            at = pl.ds(first, many)
            crossed_copies[h, d] = send(
                part.at[h, other, at], crossed.at[h, at], x_send.at[h, d], x_recv.at[h, d],
                {"dev_2": other},
            )

    holding = {}

    def collect(k):
        distance = half_n + 1 - k
        for h in range(2):
            crossed_copies[h, distance].wait_recv()
        for g in (2, 1, 0):
            low, count = GROUPS_OF_BLOCKS[g]
            at = pl.ds(low, count)
            for h in range(2):
                for way, steps, turn in ways:
                    s = k - (half_n - steps)
                    if s < 1:
                        continue
                    slot = slot_at(turn, distance)
                    total = part[h, core, slot, at].astype(jnp.float32) + crossed[h, slot, at].astype(
                        jnp.float32
                    )
                    if s > 1:
                        holding[h, way, s - 1, g].wait_recv()
                        total = total + hops[h, way, s - 2, at].astype(jnp.float32)
                    part[h, core, slot, at] = total.astype(jnp.bfloat16)
                    holding[h, way, s, g] = send(
                        part.at[h, core, slot, at], hops.at[h, way, s - 1, at],
                        r_send.at[h, way, s - 1, g], r_recv.at[h, way, s - 1, g],
                        {RING[h]: wrap(pos[h] + turn)},
                    )

    def collect_own(g):
        low, count = GROUPS_OF_BLOCKS[g]
        at = pl.ds(low, count)
        for h in range(2):
            total = part[h, core, 0, at].astype(jnp.float32) + crossed[h, 0, at].astype(jnp.float32)
            for way, steps, turn in ways:
                holding[h, way, steps, g].wait_recv()
                total = total + hops[h, way, steps - 1, at].astype(jnp.float32)
            part[h, core, 0, at] = total.astype(jnp.bfloat16)
        for slot in reversed(range(max(low, 1), low + count)):
            for h in range(2):
                finals.append(
                    send(
                        part.at[h, core, 0, slot], fin.at[h, slot], f_send.at[h, slot], f_recv.at[h, slot],
                        {LINE[h]: wrap(line[h] + OFFSETS[slot])},
                    )
                )

    finals = []
    descend(4)
    descend(3)
    collect(1)
    descend(2)
    collect(2)
    descend(1)
    collect(3)
    descend(0)
    collect(4)
    for h in range(2):
        crossed_copies[h, 0].wait_recv()
    collect_own(2)
    collect_own(1)
    collect_own(0)
    for copy in finals:
        copy.wait_recv()
    totals = []
    for h in range(2):
        total = part[h, core, 0, 0].astype(jnp.float32)
        for slot in range(1, n):
            total = total + fin[h, slot].astype(jnp.float32)
        totals.append(total)
    moe = jnp.concatenate(totals, 1)
    pieces = []
    for i in range(2):
        pieces.append(moe[8 * i : 8 * i + 8])
        pieces.append(pltpu.roll(moe[8 * i : 8 * i + 8], reqs, 0))
    final = hidden8[...] + jnp.concatenate(pieces, 1)
    out_ref[...] = final[0:reqs]
    for copy in pending:
        copy.wait_send()


def per_device(
    tokens,
    queries,
    token_kv,
    kv_cache,
    context_lengths,
    fresh_kv,
    block_counts,
    expert_ids,
    route_weights,
    norm_gain,
    w_gate,
    w_up,
    w_down,
):
    n = lax.axis_size("dev_0")
    reqs, full = tokens.shape
    width = full // 8
    units = w_gate.shape[1]
    rows = 2 * n * n * reqs
    size = 4 * 2 * n * reqs
    vmem = pl.BlockSpec(memory_space=pltpu.VMEM)
    anyspace = pl.BlockSpec(memory_space=pl.ANY)
    bf = jnp.bfloat16
    f32 = jnp.float32
    dma = pltpu.SemaphoreType.DMA
    half_n = n // 2
    keys = reqs * kv_cache.shape[1] + 2 * fresh_kv.shape[0] + 128
    result = pl.pallas_call(
        layer_kernel,
        out_shape=jax.ShapeDtypeStruct(tokens.shape, f32),
        in_specs=[anyspace] * 13,
        out_specs=vmem,
        scratch_shapes=[
            pltpu.VMEM((1, reqs), jnp.int32),
            pltpu.VMEM((2, reqs), jnp.int32),
            pltpu.VMEM((2, reqs), f32),
            pltpu.VMEM(tokens.shape, bf),
            pltpu.VMEM(queries.shape, bf),
            pltpu.VMEM(token_kv.shape, bf),
            pltpu.VMEM((1, block_counts.shape[0]), jnp.int32),
            pltpu.VMEM((1, full), f32),
            pltpu.VMEM((2 * reqs, full), f32),
            pltpu.VMEM((2 * reqs, full), f32),
            pltpu.VMEM((16, token_kv.shape[1]), f32),
            pltpu.VMEM((2 * reqs, full), f32),
            pltpu.VMEM((keys, token_kv.shape[1]), bf),
            pltpu.VMEM((1, 128), f32),
            pltpu.VMEM((size, size), bf),
            pltpu.VMEM((size, size), bf),
            pltpu.VMEM((2, 2, 2, n, n, 8, width), bf),
            pltpu.VMEM((2, n, n, 1, 128), f32),
            pltpu.VMEM((n, n, 8, 128), f32),
            pltpu.VMEM((4 * n * reqs, full // 2), bf),
            pltpu.VMEM((2, rows, 2 * units), f32),
            pltpu.VMEM((n, n, 8, units), f32),
            pltpu.VMEM((2, 2, n, n, 16, width), bf),
            pltpu.VMEM((2, n, n, 16, width), bf),
            pltpu.VMEM((2, 2, half_n, n, 16, width), bf),
            pltpu.VMEM((2, n, 16, width), bf),
            pltpu.VMEM((2, full // 2, 2 * units), bf),
            pltpu.VMEM(w_down.shape, bf),
            dma((17,)),
            dma((reqs + 1,)),
            dma((8,)),
            dma((1,)), dma((1,)),
            dma((2 * n,)), dma((2 * n,)),
            dma((2, 2, n)), dma((2, 2, n)),
            dma((2, 2, 2, half_n, 2)), dma((2, 2, 2, half_n, 2)),
            dma((2, 2, half_n + 1, 2)), dma((2, 2, half_n + 1, 2)),
            dma((2, half_n + 1)), dma((2, half_n + 1)),
            dma((2, 2, half_n, 3)), dma((2, 2, half_n, 3)),
            dma((2, n)), dma((2, n)),
        ],
        compiler_params=pltpu.CompilerParams(
            collective_id=0, has_side_effects=True, vmem_limit_bytes=60 * 1024 * 1024
        ),
    )(
        context_lengths.reshape(1, -1), expert_ids.T, route_weights.T, tokens, queries, token_kv,
        block_counts.reshape(1, -1), norm_gain.reshape(1, -1),
        kv_cache, fresh_kv, w_gate, w_up, w_down,
    )
    return result.astype(bf)


def solution(mesh):
    split = Mesh(
        mesh.devices.reshape(mesh.shape["groups"], 8, 8, 2), ("groups", "dev_0", "dev_1", "dev_2")
    )
    return jax.shard_map(
        per_device,
        mesh=split,
        in_specs=(
            P(GROUPS_DEV, None),
            P(GROUPS_DEV, None),
            P(GROUPS_DEV, None),
            P(GROUPS_DEV, None, None),
            P(GROUPS_DEV),
            P(GROUPS_DEV, None),
            P("groups"),
            P(GROUPS_DEV, None),
            P(GROUPS_DEV, None),
            P(),
            P(None, DEV),
            P(None, DEV),
            P(DEV, None),
        ),
        out_specs=P(GROUPS_DEV, None),
        check_vma=False,
    )
```

time: 102 us -> 89.2 us (0.87)
  Pallas kernels: 96.9 us -> 87.5 us
  local copies, waits for them, and re-layouts: 4.12 us -> 0 us
    pallas_call x1, Pallas kernels: 96.9 us -> 87.5 us  [per_device(): pl.pallas_call(layer_kernel, out_shape=jax.ShapeDtypeStruct(tokens.shape,...]
    unnamed x3 -> x0, local copies, waits for them, and re-layouts: 4.12 us -> none
where the time goes in v3:
time: 89.2 us; the launch traced here: 89.1 us
  Pallas kernels  87.5 us (98%)
  other arithmetic  1.53 us (2%)
    pallas_call x1, Pallas kernels, per_device(): pl.pallas_call(layer_kernel, out_shape=jax.ShapeDtypeStruct(tokens.shape,...  87.5 us

profile of v3, /device:TPU:516, one launch (start us, length us, event | category | flops | bytes accessed | tf_op | source)
XLA Modules:
  0.0 89.1 jit_solution(17396068253520224878)
XLA Ops:
  0.0 87.5 %shard_map.127 = f32[4,6144]{1,0:T(4,128)} custom-call(s32[1,4]{1,0:T(1,128)} %bitcast.8, s32[2,4]{1,0:T(2,128)} %bitcast.6, f32[2,4]{1,0:T(2,128)} %bitcast.7, bf16[4,6144]{1,0:T(4,128)(2,1)} %tokens_hbm.1, bf16[4,6144]{1,0:T(4,128)(2,1)} %queries_hbm.1, bf16[4,2048]{1,0:T(4,128)(2,1)} %own_hbm.1, s32[1,128]{1,0:T(1,128)} %bitcast.9, f32[1,6144]{1,0:T(1,128)} %bitcast.5, ...), custom_call_target="tpu_custom_call" | custom-call | tf_op jit(solution)/shard_map/pallas_call | solution.py:580
  87.5 1.5 %convert_element_type.3 = bf16[4,6144]{1,0:T(4,128)(2,1)} convert(f32[4,6144]{1,0:T(4,128)} %shard_map.127) | non-fusion elementwise | flops 24576 | bytes 147456 | tf_op jit(solution)/shard_map/convert_element_type | solution.py:634

commit v4 on v3

--- a/solution.py
+++ b/solution.py
@@ -102,7 +102,7 @@
     return jnp.concatenate(parts, 1)
 
 
-def attend_window(counts_ref, queries, states, kv_all, me, reqs, span, held):
+def attend_window(counts_ref, queries, states, kv_all, me, reqs, span, held, values_here):
     half = KVH * HD
     rows = queries[0].shape[0]
     counts = counts_ref[...]
@@ -114,7 +114,7 @@
     place = lax.broadcasted_iota(jnp.int32, (rows, 2 * span), 1)
     row = lax.rem(lax.broadcasted_iota(jnp.int32, (rows, 2 * span), 0), reqs)
     live = (row == 0) & (place >= first) & (place < stop)
-    parts = []
+    weights = []
     for k in range(KVH):
         top, total, mixed = states[k]
         s = scores_of(queries[k], kv_all[held : held + 2 * span, k * HD : (k + 1) * HD])
@@ -123,8 +123,13 @@
         fade = jnp.exp(top - new)
         e = jnp.exp(s - new)
         total = total * fade + jnp.sum(e, 1, keepdims=True)
-        mixed = mixed * fade + jnp.dot(
-            e.astype(jnp.bfloat16),
+        weights.append((e.astype(jnp.bfloat16), mixed * fade, total))
+    values_here()
+    parts = []
+    for k in range(KVH):
+        e, mixed, total = weights[k]
+        mixed = mixed + jnp.dot(
+            e,
             kv_all[held : held + 2 * span, half + k * HD : half + (k + 1) * HD],
             preferred_element_type=jnp.float32,
         )
@@ -238,10 +243,15 @@
         pending.append(copy)
         return copy
 
-    following = send(
-        kv_all.at[pl.ds(held, span)], kv_all.at[pl.ds(held + span, span)], win_send.at[0], win_recv.at[0],
-        place_of(me - 1),
-    )
+    columns = KVH * HD
+    following = [
+        send(
+            kv_all.at[pl.ds(held, span), pl.ds(i * columns, columns)],
+            kv_all.at[pl.ds(held + span, span), pl.ds(i * columns, columns)],
+            win_send.at[i], win_recv.at[i], place_of(me - 1),
+        )
+        for i in range(2)
+    ]
     static_slot = {o % n: i for i, o in enumerate(OFFSETS)}
     coefs[core, 0, 0] = coef_row[...]
     coef_firsts = [
@@ -297,7 +307,7 @@
     passing = {}
 
     def depart(wave):
-        for slot in range(1, n):
+        for slot in range(1, n) if wave == 0 else range(n - 1, 0, -1):
             for h in range(2):
                 offset = OFFSETS[slot]
                 passing[wave, h, slot] = send(
@@ -310,9 +320,9 @@
     early = heads_aside([mixed / total for _, total, mixed in states], reqs)
     put(0, normed_of(token + early))
     depart(0)
-    following.wait_recv()
+    following[0].wait_recv()
     hidden = token + attend_window(
-        counts_ref, queries, states, kv_all, me, reqs, span, held
+        counts_ref, queries, states, kv_all, me, reqs, span, held, following[1].wait_recv
     )
     hidden8[...] = hidden
     put(1, normed_of(hidden))
@@ -387,21 +397,29 @@
         for j in range(1, n)
     ]
     go_round(0, 2, 0)
-    arrive(1, 0)
-    go_round(1, 1, 0)
     go_round(0, 2, 1)
     arrive(1, 1)
     go_round(1, 1, 1)
+    arrive(1, 0)
+    go_round(1, 1, 0)
+    go_round(0, 3, 0)
+    go_round(0, 3, 1)
+    go_round(1, 2, 1)
+    go_round(1, 2, 0)
+    project(0)
+    go_round(0, 4, 0)
+    go_round(0, 4, 1)
+    go_round(1, 3, 1)
+    go_round(1, 3, 0)
+    project(1)
     for copy in coef_seconds:
         copy.wait_recv()
     coef_both = send(coefs.at[core], coefs.at[core], c_send.at[0], c_recv.at[0], {"dev_2": other})
-    go_round(0, 3, 0)
-    go_round(1, 2, 0)
-    project(0)
-    go_round(0, 3, 1)
-    go_round(1, 2, 1)
-    go_round(0, 4, 0)
-    go_round(1, 3, 0)
+    go_round(0, 5, 0)
+    go_round(0, 5, 1)
+    go_round(1, 4, 1)
+    go_round(1, 4, 0)
+    project(2)
     coef_both.wait_recv()
     expert = me // (devices // EXPERTS)
     row8 = lax.broadcasted_iota(jnp.int32, (8, 128), 0)
@@ -413,17 +431,9 @@
             coef_cols[r, c] = jnp.broadcast_to(
                 jnp.sum(jnp.where(keep, both, 0.0), 1, keepdims=True), (8, 128)
             )
-    project(1)
-    go_round(0, 4, 1)
-    go_round(1, 3, 1)
-    go_round(0, 5, 0)
-    go_round(1, 4, 0)
-    project(2)
-    go_round(0, 5, 1)
-    go_round(1, 4, 1)
+    go_round(1, 5, 1)
+    project(3)
     go_round(1, 5, 0)
-    project(3)
-    go_round(1, 5, 1)
     project(4)
 
     for r in range(n):
@@ -614,7 +624,7 @@
             dma((17,)),
             dma((reqs + 1,)),
             dma((8,)),
-            dma((1,)), dma((1,)),
+            dma((2,)), dma((2,)),
             dma((2 * n,)), dma((2 * n,)),
             dma((2, 2, n)), dma((2, 2, n)),
             dma((2, 2, 2, half_n, 2)), dma((2, 2, 2, half_n, 2)),

time: 89.2 us -> 90.4 us (1.013); the launches traced: 89.1 us -> 89 us
  no operation moved by 1% of the time
where the time goes in v4:
time: 90.4 us; the launch traced here: 89 us
  Pallas kernels  87.5 us (97%)
  other arithmetic  1.53 us (2%)
    pallas_call x1, Pallas kernels, per_device(): pl.pallas_call(layer_kernel, out_shape=jax.ShapeDtypeStruct(tokens.shape,...  87.5 us

profile of v4, /device:TPU:516, one launch (start us, length us, event | category | flops | bytes accessed | tf_op | source)
XLA Modules:
  0.0 89.0 jit_solution(3515286585172489737)
XLA Ops:
  0.0 87.5 %shard_map.127 = f32[4,6144]{1,0:T(4,128)} custom-call(s32[1,4]{1,0:T(1,128)} %bitcast.8, s32[2,4]{1,0:T(2,128)} %bitcast.6, f32[2,4]{1,0:T(2,128)} %bitcast.7, bf16[4,6144]{1,0:T(4,128)(2,1)} %tokens_hbm.1, bf16[4,6144]{1,0:T(4,128)(2,1)} %queries_hbm.1, bf16[4,2048]{1,0:T(4,128)(2,1)} %own_hbm.1, s32[1,128]{1,0:T(1,128)} %bitcast.9, f32[1,6144]{1,0:T(1,128)} %bitcast.5, ...), custom_call_target="tpu_custom_call" | custom-call | tf_op jit(solution)/shard_map/pallas_call | solution.py:590
  87.5 1.5 %convert_element_type.3 = bf16[4,6144]{1,0:T(4,128)(2,1)} convert(f32[4,6144]{1,0:T(4,128)} %shard_map.127) | non-fusion elementwise | flops 24576 | bytes 147456 | tf_op jit(solution)/shard_map/convert_element_type | solution.py:644
